TPU v7x, 32 devices: a whole 2x2x4 slice. The times are simulated.
32 devices in a mesh: dp: 32 (over z, y, x, core).
Axes of the slice: x: 2, y: 2, z: 4, core: 2. Of those that a mesh axis runs over, the one named last changes fastest.
Arguments:
- query_features: bfloat16 [8192, 768], P('dp'), may hold values from -24 to 24
- passage_features: bfloat16 [8192, 768], P('dp'), may hold values from -24 to 24
- counts: int32 [32], replicated, may hold values from 128 to 256, as said below
- positives: int32 [8192], P('dp'), may hold values from 0 to 4351
- w_first: bfloat16 [768, 1536], replicated, may hold values from -0.21875 to 0.21875
- w_second: bfloat16 [1536, 384], replicated, may hold values from -0.15625 to 0.15625
Outputs:
- mean_loss: float32 [], replicated
- grad_first: float32 [768, 1536], P(None, 'dp')
- grad_second: float32 [1536, 384], P('dp')
Inputs may be any that keep to these rules, and one draw needn't show every extreme that they name: Device i holds counts[i] pairs in the first slots of its 256 slots. Each entry is 128 or 256; among the 16 devices whose indices agree modulo 32 // 16 exactly one entry is 256, so the entries sum to 4352. `positives`: only entries of occupied slots are used; an entry is the index of a passage in the order of occupied slots, device by device.
All inputs are finite; a program needn't handle non-finite values.
Results may differ from a plain program's by a relative error of at most 0.0043.
The roundings to bfloat16 on the way count: a program that leaves them out, or rounds other values in their place, can miss the bound.
Values may be sent and summed in bfloat16 or wider, within the bound.
A program may use at most 128 MiB of HBM per device.

v0:
```python
import functools

import jax
import jax.numpy as jnp
from jax import lax
from jax.experimental import pallas as pl
from jax.experimental.pallas import tpu as pltpu
from jax.sharding import PartitionSpec as P

MESH = pl.DeviceIdType.MESH
F32 = jnp.float32
BF16 = jnp.bfloat16
GELU_ROOT = 0.7978845608028654
GELU_CUBE = 0.044715
TILES = 2


def gelu_and_slope(value):
    square = value * value
    bent = jnp.tanh(GELU_ROOT * value * (1.0 + GELU_CUBE * square))
    rise = 0.5 * (1.0 + bent)
    slope = rise + 0.5 * value * (1.0 - bent * bent) * (
        GELU_ROOT * (1.0 + 3.0 * GELU_CUBE * square)
    )
    return value * rise, slope


def dot(left, right, left_dim, right_dim):
    return lax.dot_general(
        left, right, (((left_dim,), (right_dim,)), ((), ())), preferred_element_type=F32
    )


def flat_rows(blocks):
    return blocks.astype(F32).reshape(-1, blocks.shape[-1]).astype(BF16)


class Copies:
    def __init__(self, send, recv):
        self.send, self.recv, self.used = send, recv, 0

    def start(self, source, landing, device):
        copy = pltpu.make_async_remote_copy(
            src_ref=source,
            dst_ref=landing,
            send_sem=self.send.at[self.used],
            recv_sem=self.recv.at[self.used],
            device_id=(device,),
            device_id_type=MESH,
        )
        self.used += 1
        copy.start()
        return copy


def wait_all(copies):
    for copy in copies:
        copy.wait()


def step_kernel(
    size,
    plane,
    score_scale,
    counts,
    query_features,
    passage_features,
    positives,
    w_first_hbm,
    w_second_hbm,
    out_loss,
    out_all,
    units,
    unit_mid,
    unit_pass,
    unit_land,
    unit_pos,
    feat_base,
    feat_tail,
    q_base,
    q_tail,
    p_base,
    p_tail,
    pos_land,
    all_q,
    all_p,
    scores,
    stat_land,
    dq_own_base,
    dq_own_tail,
    dq_out_base,
    dq_out_tail,
    dq_land_base,
    dq_land_tail,
    dp_own_base,
    dp_own_tail,
    dp_out_base,
    dp_out_tail,
    dp_land_base,
    dp_land_tail,
    loss_land,
    de_base,
    de_tail,
    all_x,
    own,
    outgoing,
    landing,
    sums,
    forward,
    landed,
    send_sems,
    recv_sems,
    line_send,
    line_recv,
    w_first,
    w_second,
    all_hidden,
    all_slope,
    load_sems,
):
    me = lax.axis_index("dp")
    loads = [
        pltpu.make_async_copy(w_first_hbm, w_first, load_sems.at[0]),
        pltpu.make_async_copy(w_second_hbm, w_second, load_sems.at[1]),
    ]
    for load in loads:
        load.start()
    rows = size // plane
    half = rows // 2
    lanes = plane // 2
    stride = size // 16
    row = lax.div(me, plane)
    spot = lax.rem(me, plane)
    core = lax.rem(me, 2)
    lane = lax.div(spot, 2)
    column = spot - core
    place = lax.div(me, stride)
    partner = me + 1 - 2 * core
    width, hidden_width = w_first.shape
    embed = w_second.shape[1]
    base = q_base.shape[1]
    unit = q_tail.shape[1]
    hidden_half = hidden_width // 2
    tile = hidden_half // TILES
    per_tile = half // TILES
    chunk = hidden_half // (half * lanes * 2)
    copies = Copies(send_sems, recv_sems)

    plane_peers = [row * plane + lax.rem(spot + k, plane) for k in range(1, plane)]
    line_peers = [lax.rem(row + k, rows) * plane + spot for k in range(1, rows)]
    barrier = pltpu.get_barrier_semaphore()

    def greet(device):
        pl.semaphore_signal(barrier, inc=1, device_id=(device,), device_id_type=MESH)

    for k in range(1, 16):
        greet(lax.rem(place + k, 16) * stride + lax.rem(me, stride))
    for device in plane_peers:
        greet(device)
    in_column = 2 * row + core
    for k in range(1, 2 * rows):
        other = lax.rem(in_column + k, 2 * rows)
        greet(plane * lax.div(other, 2) + column + lax.rem(other, 2))

    spare = base + unit
    near = plane // stride
    aside = lax.div(spot, stride)
    extra_q = query_features[spare:].astype(F32).reshape(15, unit, width).astype(BF16)
    extra_p = passage_features[spare:].astype(F32).reshape(15, unit, width).astype(BF16)
    for u in range(15):
        there = u + lax.div(u + 16 - place, 16)
        units[lax.div(there, near), lax.rem(there, near), :, :width] = extra_q[u]
        units[lax.div(there, near), lax.rem(there, near), :, width:] = extra_p[u]
    unit_pos[place] = positives[...].astype(F32)

    pl.semaphore_wait(barrier, 15 + plane - 1 + 2 * rows - 1)

    mid_copies = []
    for k in range(1, near):
        there = lax.rem(aside + k, near)
        mid_copies.append(
            copies.start(
                units.at[:, there],
                unit_mid.at[aside],
                row * plane + there * stride + lax.rem(me, stride),
            )
        )
    unit_copies = []
    for k in range(1, 16):
        device = lax.rem(place + k, 16) * stride + lax.rem(me, stride)
        unit_copies.append(copies.start(unit_pos.at[place], unit_pos.at[place], device))

    heavies = []
    for g in range(stride):
        at = jnp.int32(0)
        for k in range(16):
            at = at + jnp.where(counts[g + stride * k] > base, g + stride * k, 0)
        heavies.append(at)
    source = jnp.int32(0)
    for g in range(stride):
        source = source + jnp.where(lax.rem(me, stride) == g, heavies[g], 0)
    heavy_place = jnp.int32(0)
    for k in range(16):
        heavy_place = heavy_place + jnp.where(source >= stride * (k + 1), 1, 0)

    def offset_of(device):
        before = jnp.int32(0)
        for at in heavies:
            before = before + jnp.where(at < device, 1, 0)
        return base * (device + before)

    def tail_row(device):
        piece = lax.div(device, stride) - jnp.where(source < device, 1, 0)
        return jnp.where(source == device, base, spare + unit * piece)

    def tower(features):
        total = None
        for low in range(0, hidden_width, tile):
            act = dot(features, w_first[:, low : low + tile], 1, 0)
            hidden = gelu_and_slope(act)[0].astype(BF16)
            part = dot(hidden, w_second[low : low + tile, :], 1, 0)
            total = part if total is None else total + part
        return total.astype(BF16)

    feat_base[core, 0] = query_features[:base]
    feat_base[core, 1] = passage_features[:base]
    pair_x = [copies.start(feat_base.at[core], feat_base.at[core], partner)]
    wait_all(loads)
    embedded = tower(feat_base[core].reshape(2 * base, width))
    q_base[spot] = embedded[:base]
    p_base[row] = embedded[base:]
    q_copies = [copies.start(q_base.at[spot], q_base.at[spot], device) for device in plane_peers]
    wait_all(mid_copies)
    source_row, source_aside = jnp.int32(0), heavy_place
    for k in range(1, rows):
        beyond = heavy_place >= k * near
        source_row = source_row + jnp.where(beyond, 1, 0)
        source_aside = source_aside - jnp.where(beyond, near, 0)
    unit_pass[...] = jnp.where(source_aside == aside, units[:, aside], unit_mid[source_aside])
    for k in range(1, rows):
        there = lax.rem(row + k, rows)
        unit_copies.append(
            copies.start(unit_pass.at[there], unit_land.at[row], there * plane + spot)
        )
    p_copies = [copies.start(p_base.at[row], p_base.at[row], device) for device in line_peers]

    wait_all(unit_copies)
    heavy = source == me
    got = jnp.where(source_row == row, unit_pass[row], unit_land[source_row]).astype(F32)
    tail_q = jnp.where(heavy, query_features[base:spare].astype(F32), got[:, :width])
    tail_p = jnp.where(heavy, passage_features[base:spare].astype(F32), got[:, width:])
    slots = lax.broadcasted_iota(jnp.int32, (unit, positives.shape[1]), 1)
    chosen = lax.broadcasted_iota(jnp.int32, slots.shape, 0) + tail_row(me)
    tail_pos = jnp.sum(
        jnp.where(slots == chosen, unit_pos[heavy_place], 0.0), axis=1, keepdims=True
    )
    tail_x = jnp.concatenate([tail_q, tail_p], axis=0)
    feat_tail[core] = tail_x.reshape(2, unit, width).astype(BF16)
    tail_e = tower(tail_x.astype(BF16)).astype(F32)
    q_tail[spot] = tail_e[:unit].astype(BF16)
    p_tail[row] = tail_e[unit:].astype(BF16)
    pos_land[spot, 0] = positives[:, :base].astype(F32)
    sub = lax.broadcasted_iota(jnp.int32, (unit, base), 0) + spot * unit
    along = lax.broadcasted_iota(jnp.int32, (unit, base), 1)
    pos_land[spot, 1] = jnp.sum(jnp.where(sub == along, tail_pos, 0.0), axis=0, keepdims=True)
    for device in plane_peers:
        q_copies.append(copies.start(pos_land.at[spot], pos_land.at[spot], device))
        q_copies.append(copies.start(q_tail.at[spot], q_tail.at[spot], device))
    for device in line_peers:
        p_copies.append(copies.start(p_tail.at[row], p_tail.at[row], device))
    pair_x.append(copies.start(feat_tail.at[core], feat_tail.at[core], partner))
    wait_all(q_copies)
    wait_all(p_copies)

    q_rows, p_rows = plane * base, rows * base
    all_q[:q_rows] = q_base[...].reshape(q_rows, embed)
    all_q[q_rows:] = flat_rows(q_tail[...])
    all_p[:p_rows] = p_base[...].reshape(p_rows, embed)
    all_p[p_rows:] = flat_rows(p_tail[...])
    pos_tail = pos_land[0, 1]
    for k in range(1, plane):
        pos_tail = pos_tail + pos_land[k, 1]
    wanted = jnp.concatenate(
        [pos_land[k, 0] for k in range(plane)] + [pos_tail[:, : plane * unit]], axis=1
    )
    line = [plane * k + spot for k in range(rows)]
    ids = jnp.concatenate(
        [lax.broadcasted_iota(jnp.int32, (base, 1), 0) + offset_of(device) for device in line]
        + [
            lax.broadcasted_iota(jnp.int32, (unit, 1), 0) + offset_of(source) + tail_row(device)
            for device in line
        ],
        axis=0,
    ).astype(F32)
    scores[...] = score_scale * dot(all_p[...], all_q[...], 1, 1)
    value = scores[...]
    hit = ids == wanted
    top = jnp.max(value, axis=0, keepdims=True)
    stat_land[spot, 0:1] = top
    stat_land[spot, 1:2] = jnp.sum(jnp.exp(value - top), axis=0, keepdims=True)
    stat_land[spot, 2:3] = jnp.sum(jnp.where(hit, value, 0.0), axis=0, keepdims=True)
    stat_land[spot, 3:4] = jnp.zeros_like(top)
    wait_all(
        [copies.start(stat_land.at[spot], stat_land.at[spot], device) for device in plane_peers]
    )
    stats = stat_land[...]
    tops = stats[:, 0]
    row_top = jnp.max(tops, axis=0, keepdims=True)
    mass = jnp.sum(stats[:, 1] * jnp.exp(tops - row_top), axis=0, keepdims=True)
    log_norm = row_top + jnp.log(mass)
    found = jnp.sum(stats[:, 2], axis=0, keepdims=True)
    loss_land[row] = jnp.broadcast_to(
        jnp.sum(log_norm - found, axis=1, keepdims=True), loss_land.shape[1:]
    )
    grads_t = (jnp.exp(scores[...] - log_norm) - hit.astype(F32)).astype(BF16)

    def scatter(part, own_base, own_tail, out_base, out_tail, land_base, land_tail, mine, peers):
        split = own_base.shape[0] * base
        own_base[...] = part[:split].reshape(own_base.shape)
        own_tail[...] = part[split:].reshape(own_tail.shape)
        out_base[...] = own_base[...].astype(out_base.dtype)
        out_tail[...] = own_tail[...].astype(out_tail.dtype)
        made = []
        for there, device in peers:
            made.append(copies.start(out_base.at[there], land_base.at[mine], device))
            made.append(copies.start(out_tail.at[there], land_tail.at[mine], device))
        return made

    def gathered(own_part, land, mine, members):
        total = own_part[mine]
        for k in range(1, members):
            total = total + land[lax.rem(mine + k, members)].astype(F32)
        return total.astype(BF16)

    dq_copies = scatter(
        score_scale * dot(grads_t, all_p[...], 0, 0),
        dq_own_base,
        dq_own_tail,
        dq_out_base,
        dq_out_tail,
        dq_land_base,
        dq_land_tail,
        spot,
        [(lax.rem(spot + k, plane), plane_peers[k - 1]) for k in range(1, plane)],
    )
    dp_copies = scatter(
        score_scale * dot(grads_t, all_q[...], 1, 0),
        dp_own_base,
        dp_own_tail,
        dp_out_base,
        dp_out_tail,
        dp_land_base,
        dp_land_tail,
        row,
        [(lax.rem(row + k, rows), line_peers[k - 1]) for k in range(1, rows)],
    )
    loss_copies = [
        copies.start(loss_land.at[row], loss_land.at[row], device) for device in line_peers
    ]
    wait_all(pair_x)
    x_rows = 4 * base
    all_x[:x_rows] = feat_base[...].reshape(x_rows, width)
    all_x[x_rows:] = flat_rows(feat_tail[...])
    for t in range(TILES):
        start = pl.multiple_of(core * hidden_half + t * tile, 128)
        hidden, slope = gelu_and_slope(dot(all_x[...], w_first[:, pl.ds(start, tile)], 1, 0))
        all_hidden[t] = hidden.astype(BF16)
        all_slope[t] = slope
    wait_all(dq_copies)
    de_base[core, 0] = gathered(dq_own_base, dq_land_base, spot, plane)
    de_tail[core, 0] = gathered(dq_own_tail, dq_land_tail, spot, plane)

    def send_de(side):
        return [
            copies.start(de_base.at[core, side], de_base.at[core, side], partner),
            copies.start(de_tail.at[core, side], de_tail.at[core, side], partner),
        ]

    pair_de = send_de(0)
    wait_all(dp_copies)
    de_base[core, 1] = gathered(dp_own_base, dp_land_base, row, rows)
    de_tail[core, 1] = gathered(dp_own_tail, dp_land_tail, row, rows)
    pair_de += send_de(1)
    wait_all(loss_copies)
    loss = loss_land[0]
    for k in range(1, rows):
        loss = loss + loss_land[k]
    out_loss[...] = loss * (1.0 / (size * spare))

    def keep(t, part, low):
        high = low + part.shape[1]
        for i in range(per_tile):
            for m in range(lanes):
                for j in range(2):
                    at = ((i * lanes + m) * 2 + j) * chunk
                    piece = part[at : at + chunk]
                    own[t * per_tile + i, m, j, :, low:high] = piece
                    outgoing[t * per_tile + i, m, j, :, low:high] = piece.astype(BF16)
        made = []
        block = pl.ds(t * per_tile, per_tile)
        for k in range(1, lanes):
            there = lax.rem(lane + k, lanes)
            made.append(
                copies.start(
                    outgoing.at[block, there, :, :, pl.ds(low, high - low)],
                    landing.at[lane, block, :, :, pl.ds(low, high - low)],
                    plane * row + 2 * there + core,
                )
            )
        return made

    wait_all(pair_de)
    de = jnp.concatenate([de_base[...].reshape(x_rows, embed), flat_rows(de_tail[...])], axis=0)
    lane_copies = [keep(0, dot(all_hidden[0], de, 0, 0), width)]
    for t in range(TILES):
        start = pl.multiple_of(core * hidden_half + t * tile, 128)
        back = dot(de, w_second[pl.ds(start, tile), :], 1, 1)
        act_grad = (all_slope[t] * back).astype(BF16)
        lane_copies[t] += keep(t, dot(act_grad, all_x[...], 0, 0), 0)
        if t + 1 < TILES:
            lane_copies.append(keep(t + 1, dot(all_hidden[t + 1], de, 0, 0), width))

    sender_core = lax.div(row, half)

    def line_copy(i, j):
        return pltpu.make_async_remote_copy(
            src_ref=forward.at[i, j],
            dst_ref=landed.at[row],
            send_sem=line_send.at[i, j],
            recv_sem=line_recv.at[row],
            device_id=(plane * (half * core + i) + column + j,),
            device_id_type=MESH,
        )

    for t in range(TILES):
        wait_all(lane_copies[t])
        for i in range(t * per_tile, (t + 1) * per_tile):
            for j in range(2):
                total = own[i, lane, j]
                for k in range(1, lanes):
                    total = total + landing[lax.rem(lane + k, lanes), i, j].astype(F32)
                sums[i, j] = total
                forward[i, j] = total.astype(BF16)

                @pl.when(plane * (half * core + i) + column + j != me)
                def _():
                    line_copy(i, j).start()

    for i in range(half):
        for j in range(2):

            @pl.when(plane * (half * core + i) + column + j != me)
            def _():
                line_copy(i, j).wait_send()

    for sender_row in range(rows):
        sender = plane * sender_row + column + sender_core

        @pl.when(sender != me)
        def _():
            pltpu.make_async_remote_copy(
                src_ref=forward.at[0, 0],
                dst_ref=landed.at[sender_row],
                send_sem=line_send.at[0, 0],
                recv_sem=line_recv.at[sender_row],
                device_id=(sender,),
                device_id_type=MESH,
            ).wait_recv()

    total = jnp.where(sender_core == core, sums[lax.rem(row, half), core], 0.0)
    for sender_row in range(rows):
        sender = plane * sender_row + column + sender_core
        total = total + jnp.where(sender == me, 0.0, landed[sender_row].astype(F32))
    out_all[...] = total


def split_kernel(loss, total, mean_loss, first, second):
    width = first.shape[1]
    mean_loss[0] = loss[0, 0]
    first[...] = total[:, :width]
    second[...] = total[:, width:]


def split_outputs(loss, total, width):
    vmem = pl.BlockSpec(memory_space=pltpu.VMEM)
    chunk, across = total.shape
    return pl.pallas_call(
        split_kernel,
        out_shape=[
            jax.ShapeDtypeStruct((1,), F32),
            jax.ShapeDtypeStruct((chunk, width), F32),
            jax.ShapeDtypeStruct((chunk, across - width), F32),
        ],
        in_specs=[pl.BlockSpec(memory_space=pltpu.SMEM), vmem],
        out_specs=[pl.BlockSpec(memory_space=pltpu.SMEM), vmem, vmem],
    )(loss, total)


def step(size, plane, score_scale, counts, *arrays):
    query_features, _, positives, w_first, w_second = arrays
    rows, lanes = size // plane, plane // 2
    half = rows // 2
    width, hidden_width = w_first.shape
    embed = w_second.shape[1]
    chunk = hidden_width // size
    across = width + embed
    base = query_features.shape[0] // 2
    unit = base // 16
    block = base + unit
    vmem = pl.BlockSpec(memory_space=pltpu.VMEM)
    count = 30 + 4 * (plane - 1) + 2 * (rows - 1) + 2
    count += 2 * (plane - 1) + 3 * (rows - 1) + 4 + 2 * TILES * (lanes - 1)

    def split(members, dtype):
        return [
            pltpu.VMEM((members, base, embed), dtype),
            pltpu.VMEM((members, unit, embed), dtype),
        ]

    scratch = [
        pltpu.VMEM((rows, 16 // rows, unit, 2 * width), BF16),
        pltpu.VMEM((16 // rows, rows, unit, 2 * width), BF16),
        pltpu.VMEM((rows, unit, 2 * width), BF16),
        pltpu.VMEM((rows, unit, 2 * width), BF16),
        pltpu.VMEM((16,) + positives.shape, F32),
        pltpu.VMEM((2, 2, base, width), BF16),
        pltpu.VMEM((2, 2, unit, width), BF16),
        *split(plane, BF16),
        *split(rows, BF16),
        pltpu.VMEM((plane, 2, 1, base), F32),
        pltpu.VMEM((plane * block, embed), BF16),
        pltpu.VMEM((rows * block, embed), BF16),
        pltpu.VMEM((rows * block, plane * block), F32),
        pltpu.VMEM((plane, 4, plane * block), F32),
        *split(plane, F32),
        *split(plane, BF16),
        *split(plane, BF16),
        *split(rows, F32),
        *split(rows, BF16),
        *split(rows, BF16),
        pltpu.VMEM((rows, 8, 128), F32),
        pltpu.VMEM((2, 2, base, embed), BF16),
        pltpu.VMEM((2, 2, unit, embed), BF16),
        pltpu.VMEM((4 * block, width), BF16),
        pltpu.VMEM((half, lanes, 2, chunk, across), F32),
        pltpu.VMEM((half, lanes, 2, chunk, across), BF16),
        pltpu.VMEM((lanes, half, 2, chunk, across), BF16),
        pltpu.VMEM((half, 2, chunk, across), F32),
        pltpu.VMEM((half, 2, chunk, across), BF16),
        pltpu.VMEM((rows, chunk, across), BF16),
        pltpu.SemaphoreType.DMA((count,)),
        pltpu.SemaphoreType.DMA((count,)),
        pltpu.SemaphoreType.DMA((half, 2)),
        pltpu.SemaphoreType.DMA((rows,)),
        pltpu.VMEM(w_first.shape, BF16),
        pltpu.VMEM(w_second.shape, BF16),
        pltpu.VMEM((TILES, 4 * block, hidden_width // 2 // TILES), BF16),
        pltpu.VMEM((TILES, 4 * block, hidden_width // 2 // TILES), F32),
        pltpu.SemaphoreType.DMA((2,)),
    ]
    return pl.pallas_call(
        functools.partial(step_kernel, size, plane, score_scale),
        out_shape=[
            jax.ShapeDtypeStruct((8, 128), F32),
            jax.ShapeDtypeStruct((chunk, across), F32),
        ],
        in_specs=[pl.BlockSpec(memory_space=pltpu.SMEM)] + [vmem] * 3
        + [pl.BlockSpec(memory_space=pl.ANY)] * 2,
        out_specs=[vmem] * 2,
        scratch_shapes=scratch,
        compiler_params=pltpu.CompilerParams(
            collective_id=0, has_side_effects=True, vmem_limit_bytes=60 * 1024 * 1024
        ),
    )(counts, *arrays)


def body(query_features, passage_features, counts, positives, w_first, w_second):
    device_count = lax.axis_size("dp")
    plane = 1 << device_count.bit_length() // 2
    score_scale = 2.5 * w_second.shape[1] ** (-0.5)
    loss, total = step(
        device_count,
        plane,
        score_scale,
        counts,
        query_features,
        passage_features,
        positives[None, :],
        w_first,
        w_second,
    )
    mean_loss, grad_first, grad_second = split_outputs(loss, total, w_first.shape[0])
    return (mean_loss[0], grad_first.T, grad_second)


def solution(mesh):
    return jax.shard_map(
        body,
        mesh=mesh,
        in_specs=(P("dp", None), P("dp", None), P(), P("dp"), P(), P()),
        out_specs=(P(), P(None, "dp"), P("dp", None)),
        check_vma=False,
    )
```

profile of v0, /device:TPU:9, one launch (start us, length us, event | category | flops | bytes accessed | tf_op | source)
XLA Modules:
  0.0 77.5 jit_solution(8161651718557706192)
XLA Ops:
  0.6 75.2 %shard_map.85 = (f32[8,128]{1,0:T(8,128)}, f32[48,1152]{1,0:T(8,128)}) custom-call(s32[32]{0:T(128)} %counts.1, bf16[256,768]{1,0:T(8,128)(2,1)} %query_features.1, bf16[256,768]{1,0:T(8,128)(2,1)} %passage_features.1, s32[1,256]{1,0:T(1,128)} %bitcast.3, bf16[768,1536]{1,0:T(8,128)(2,1)} %w_first_hbm.1, bf16[1536,384]{1,0:T(8,128)(2,1)} %w_second_hbm.1), custom_call_target="tpu_custom_call" | custom-call | tf_op jit(solution)/shard_map/pallas_call | solution.py:561
  75.9 1.6 %shard_map.86 = (f32[1]{0:T(128)}, f32[48,768]{1,0:T(8,128)}, f32[48,384]{1,0:T(8,128)}) custom-call(f32[8,128]{1,0:T(8,128)} %get-tuple-element.8.loss, f32[48,1152]{1,0:T(8,128)} %get-tuple-element.9.total), custom_call_target="tpu_custom_call" | custom-call | tf_op jit(solution)/shard_map/pallas_call | solution.py:487
where the time goes:
time: 77.7 us; the launch traced here: 77.5 us
  Pallas kernels  76.9 us (99%)
    pallas_call x1, Pallas kernels, step(): pl.pallas_call(functools.partial(step_kernel, size, plane, score_scale),...  75.2 us
    pallas_call x1, Pallas kernels, split_outputs(): pl.pallas_call(split_kernel, out_shape=[jax.ShapeDtypeStruct((1,), F32),...  1.65 us

commit v1 on v0

--- a/solution.py
+++ b/solution.py
@@ -13,6 +13,8 @@
 GELU_ROOT = 0.7978845608028654
 GELU_CUBE = 0.044715
 TILES = 2
+AHEAD = 3
+DELAY = 2
 
 
 def gelu_and_slope(value):
@@ -35,27 +37,38 @@
     return blocks.astype(F32).reshape(-1, blocks.shape[-1]).astype(BF16)
 
 
-class Copies:
+class Group:
+    def __init__(self, send, recv):
+        self.send, self.recv = send, recv
+
+    def start(self, source, landing, device):
+        pltpu.make_async_remote_copy(
+            src_ref=source,
+            dst_ref=landing,
+            send_sem=self.send,
+            recv_sem=self.recv,
+            device_id=(device,),
+            device_id_type=MESH,
+        ).start()
+
+    def landed(self, span):
+        pltpu.make_async_copy(span, span, self.recv).wait()
+
+    def sent(self, span):
+        pltpu.make_async_copy(span, span, self.send).wait()
+
+    def done(self, span):
+        self.landed(span)
+        self.sent(span)
+
+
+class Groups:
     def __init__(self, send, recv):
         self.send, self.recv, self.used = send, recv, 0
 
-    def start(self, source, landing, device):
-        copy = pltpu.make_async_remote_copy(
-            src_ref=source,
-            dst_ref=landing,
-            send_sem=self.send.at[self.used],
-            recv_sem=self.recv.at[self.used],
-            device_id=(device,),
-            device_id_type=MESH,
-        )
+    def new(self):
         self.used += 1
-        copy.start()
-        return copy
-
-
-def wait_all(copies):
-    for copy in copies:
-        copy.wait()
+        return Group(self.send.at[self.used - 1], self.recv.at[self.used - 1])
 
 
 def step_kernel(
@@ -63,8 +76,8 @@
     plane,
     score_scale,
     counts,
-    query_features,
-    passage_features,
+    query_hbm,
+    passage_hbm,
     positives,
     w_first_hbm,
     w_second_hbm,
@@ -101,10 +114,13 @@
     loss_land,
     de_base,
     de_tail,
+    own_tail,
     all_x,
     own,
     outgoing,
     landing,
+    outgoing_two,
+    landing_two,
     sums,
     forward,
     landed,
@@ -119,12 +135,6 @@
     load_sems,
 ):
     me = lax.axis_index("dp")
-    loads = [
-        pltpu.make_async_copy(w_first_hbm, w_first, load_sems.at[0]),
-        pltpu.make_async_copy(w_second_hbm, w_second, load_sems.at[1]),
-    ]
-    for load in loads:
-        load.start()
     rows = size // plane
     half = rows // 2
     lanes = plane // 2
@@ -144,7 +154,7 @@
     tile = hidden_half // TILES
     per_tile = half // TILES
     chunk = hidden_half // (half * lanes * 2)
-    copies = Copies(send_sems, recv_sems)
+    groups = Groups(send_sems, recv_sems)
 
     plane_peers = [row * plane + lax.rem(spot + k, plane) for k in range(1, plane)]
     line_peers = [lax.rem(row + k, rows) * plane + spot for k in range(1, rows)]
@@ -165,30 +175,52 @@
     spare = base + unit
     near = plane // stride
     aside = lax.div(spot, stride)
-    extra_q = query_features[spare:].astype(F32).reshape(15, unit, width).astype(BF16)
-    extra_p = passage_features[spare:].astype(F32).reshape(15, unit, width).astype(BF16)
-    for u in range(15):
-        there = u + lax.div(u + 16 - place, 16)
-        units[lax.div(there, near), lax.rem(there, near), :, :width] = extra_q[u]
-        units[lax.div(there, near), lax.rem(there, near), :, width:] = extra_p[u]
+    for at, (features, sem) in enumerate(((query_hbm, 0), (passage_hbm, 1))):
+        side = pl.ds(at * width, width)
+        for u in range(15):
+            there = u + lax.div(u + 16 - place, 16)
+            pltpu.make_async_copy(
+                features.at[pl.ds(spare + u * unit, unit), :],
+                units.at[lax.div(there, near), lax.rem(there, near), :, side],
+                load_sems.at[sem],
+            ).start()
+    base_loads = [
+        pltpu.make_async_copy(
+            features.at[pl.ds(0, base), :], feat_base.at[core, at], load_sems.at[2 + at]
+        )
+        for at, features in enumerate((query_hbm, passage_hbm))
+    ]
+    weight_loads = [
+        pltpu.make_async_copy(w_first_hbm, w_first, load_sems.at[4]),
+        pltpu.make_async_copy(w_second_hbm, w_second, load_sems.at[5]),
+    ]
+    tail_loads = [
+        pltpu.make_async_copy(
+            features.at[pl.ds(base, unit), :], own_tail.at[at], load_sems.at[6 + at]
+        )
+        for at, features in enumerate((query_hbm, passage_hbm))
+    ]
+    for load in base_loads + weight_loads + tail_loads:
+        load.start()
     unit_pos[place] = positives[...].astype(F32)
 
     pl.semaphore_wait(barrier, 15 + plane - 1 + 2 * rows - 1)
-
-    mid_copies = []
+    for features, sem in ((query_hbm, 0), (passage_hbm, 1)):
+        extra = features.at[pl.ds(spare, 15 * unit), :]
+        pltpu.make_async_copy(extra, extra, load_sems.at[sem]).wait()
+
+    mid_group = groups.new()
     for k in range(1, near):
         there = lax.rem(aside + k, near)
-        mid_copies.append(
-            copies.start(
-                units.at[:, there],
-                unit_mid.at[aside],
-                row * plane + there * stride + lax.rem(me, stride),
-            )
+        mid_group.start(
+            units.at[:, there],
+            unit_mid.at[aside],
+            row * plane + there * stride + lax.rem(me, stride),
         )
-    unit_copies = []
+    where_group = groups.new()
     for k in range(1, 16):
         device = lax.rem(place + k, 16) * stride + lax.rem(me, stride)
-        unit_copies.append(copies.start(unit_pos.at[place], unit_pos.at[place], device))
+        where_group.start(unit_pos.at[place], unit_pos.at[place], device)
 
     heavies = []
     for g in range(stride):
@@ -222,33 +254,40 @@
             total = part if total is None else total + part
         return total.astype(BF16)
 
-    feat_base[core, 0] = query_features[:base]
-    feat_base[core, 1] = passage_features[:base]
-    pair_x = [copies.start(feat_base.at[core], feat_base.at[core], partner)]
-    wait_all(loads)
+    for load in base_loads:
+        load.wait()
+    pair_base = groups.new()
+    pair_base.start(feat_base.at[core], feat_base.at[core], partner)
+    for load in weight_loads:
+        load.wait()
     embedded = tower(feat_base[core].reshape(2 * base, width))
     q_base[spot] = embedded[:base]
     p_base[row] = embedded[base:]
-    q_copies = [copies.start(q_base.at[spot], q_base.at[spot], device) for device in plane_peers]
-    wait_all(mid_copies)
+    q_group, p_group = groups.new(), groups.new()
+    for device in plane_peers:
+        q_group.start(q_base.at[spot], q_base.at[spot], device)
+    mid_group.done(unit_mid.at[pl.ds(0, near - 1)])
     source_row, source_aside = jnp.int32(0), heavy_place
     for k in range(1, rows):
         beyond = heavy_place >= k * near
         source_row = source_row + jnp.where(beyond, 1, 0)
         source_aside = source_aside - jnp.where(beyond, near, 0)
     unit_pass[...] = jnp.where(source_aside == aside, units[:, aside], unit_mid[source_aside])
+    pass_group = groups.new()
     for k in range(1, rows):
         there = lax.rem(row + k, rows)
-        unit_copies.append(
-            copies.start(unit_pass.at[there], unit_land.at[row], there * plane + spot)
-        )
-    p_copies = [copies.start(p_base.at[row], p_base.at[row], device) for device in line_peers]
-
-    wait_all(unit_copies)
+        pass_group.start(unit_pass.at[there], unit_land.at[row], there * plane + spot)
+    for device in line_peers:
+        p_group.start(p_base.at[row], p_base.at[row], device)
+
+    where_group.done(unit_pos.at[pl.ds(0, 15)])
+    pass_group.done(unit_land.at[pl.ds(0, rows - 1)])
+    for load in tail_loads:
+        load.wait()
     heavy = source == me
     got = jnp.where(source_row == row, unit_pass[row], unit_land[source_row]).astype(F32)
-    tail_q = jnp.where(heavy, query_features[base:spare].astype(F32), got[:, :width])
-    tail_p = jnp.where(heavy, passage_features[base:spare].astype(F32), got[:, width:])
+    tail_q = jnp.where(heavy, own_tail[0].astype(F32), got[:, :width])
+    tail_p = jnp.where(heavy, own_tail[1].astype(F32), got[:, width:])
     slots = lax.broadcasted_iota(jnp.int32, (unit, positives.shape[1]), 1)
     chosen = lax.broadcasted_iota(jnp.int32, slots.shape, 0) + tail_row(me)
     tail_pos = jnp.sum(
@@ -263,14 +302,19 @@
     sub = lax.broadcasted_iota(jnp.int32, (unit, base), 0) + spot * unit
     along = lax.broadcasted_iota(jnp.int32, (unit, base), 1)
     pos_land[spot, 1] = jnp.sum(jnp.where(sub == along, tail_pos, 0.0), axis=0, keepdims=True)
+    q_tail_group, p_tail_group, pos_group = groups.new(), groups.new(), groups.new()
     for device in plane_peers:
-        q_copies.append(copies.start(pos_land.at[spot], pos_land.at[spot], device))
-        q_copies.append(copies.start(q_tail.at[spot], q_tail.at[spot], device))
+        pos_group.start(pos_land.at[spot], pos_land.at[spot], device)
+        q_tail_group.start(q_tail.at[spot], q_tail.at[spot], device)
     for device in line_peers:
-        p_copies.append(copies.start(p_tail.at[row], p_tail.at[row], device))
-    pair_x.append(copies.start(feat_tail.at[core], feat_tail.at[core], partner))
-    wait_all(q_copies)
-    wait_all(p_copies)
+        p_tail_group.start(p_tail.at[row], p_tail.at[row], device)
+    pair_tail = groups.new()
+    pair_tail.start(feat_tail.at[core], feat_tail.at[core], partner)
+    q_group.done(q_base.at[pl.ds(0, plane - 1)])
+    q_tail_group.done(q_tail.at[pl.ds(0, plane - 1)])
+    pos_group.done(pos_land.at[pl.ds(0, plane - 1)])
+    p_group.done(p_base.at[pl.ds(0, rows - 1)])
+    p_tail_group.done(p_tail.at[pl.ds(0, rows - 1)])
 
     q_rows, p_rows = plane * base, rows * base
     all_q[:q_rows] = q_base[...].reshape(q_rows, embed)
@@ -300,9 +344,10 @@
     stat_land[spot, 1:2] = jnp.sum(jnp.exp(value - top), axis=0, keepdims=True)
     stat_land[spot, 2:3] = jnp.sum(jnp.where(hit, value, 0.0), axis=0, keepdims=True)
     stat_land[spot, 3:4] = jnp.zeros_like(top)
-    wait_all(
-        [copies.start(stat_land.at[spot], stat_land.at[spot], device) for device in plane_peers]
-    )
+    stat_group = groups.new()
+    for device in plane_peers:
+        stat_group.start(stat_land.at[spot], stat_land.at[spot], device)
+    stat_group.done(stat_land.at[pl.ds(0, plane - 1)])
     stats = stat_land[...]
     tops = stats[:, 0]
     row_top = jnp.max(tops, axis=0, keepdims=True)
@@ -320,11 +365,16 @@
         own_tail[...] = part[split:].reshape(own_tail.shape)
         out_base[...] = own_base[...].astype(out_base.dtype)
         out_tail[...] = own_tail[...].astype(out_tail.dtype)
-        made = []
+        base_group, tail_group = groups.new(), groups.new()
         for there, device in peers:
-            made.append(copies.start(out_base.at[there], land_base.at[mine], device))
-            made.append(copies.start(out_tail.at[there], land_tail.at[mine], device))
-        return made
+            base_group.start(out_base.at[there], land_base.at[mine], device)
+            tail_group.start(out_tail.at[there], land_tail.at[mine], device)
+
+        def finish():
+            base_group.done(land_base.at[pl.ds(0, len(peers))])
+            tail_group.done(land_tail.at[pl.ds(0, len(peers))])
+
+        return finish
 
     def gathered(own_part, land, mine, members):
         total = own_part[mine]
@@ -332,7 +382,7 @@
             total = total + land[lax.rem(mine + k, members)].astype(F32)
         return total.astype(BF16)
 
-    dq_copies = scatter(
+    finish_dq = scatter(
         score_scale * dot(grads_t, all_p[...], 0, 0),
         dq_own_base,
         dq_own_tail,
@@ -343,7 +393,7 @@
         spot,
         [(lax.rem(spot + k, plane), plane_peers[k - 1]) for k in range(1, plane)],
     )
-    dp_copies = scatter(
+    finish_dp = scatter(
         score_scale * dot(grads_t, all_q[...], 1, 0),
         dp_own_base,
         dp_own_tail,
@@ -354,10 +404,11 @@
         row,
         [(lax.rem(row + k, rows), line_peers[k - 1]) for k in range(1, rows)],
     )
-    loss_copies = [
-        copies.start(loss_land.at[row], loss_land.at[row], device) for device in line_peers
-    ]
-    wait_all(pair_x)
+    loss_group = groups.new()
+    for device in line_peers:
+        loss_group.start(loss_land.at[row], loss_land.at[row], device)
+    pair_base.done(feat_base.at[0])
+    pair_tail.done(feat_tail.at[0])
     x_rows = 4 * base
     all_x[:x_rows] = feat_base[...].reshape(x_rows, width)
     all_x[x_rows:] = flat_rows(feat_tail[...])
@@ -366,92 +417,175 @@
         hidden, slope = gelu_and_slope(dot(all_x[...], w_first[:, pl.ds(start, tile)], 1, 0))
         all_hidden[t] = hidden.astype(BF16)
         all_slope[t] = slope
-    wait_all(dq_copies)
+    finish_dq()
     de_base[core, 0] = gathered(dq_own_base, dq_land_base, spot, plane)
     de_tail[core, 0] = gathered(dq_own_tail, dq_land_tail, spot, plane)
 
     def send_de(side):
-        return [
-            copies.start(de_base.at[core, side], de_base.at[core, side], partner),
-            copies.start(de_tail.at[core, side], de_tail.at[core, side], partner),
-        ]
-
-    pair_de = send_de(0)
-    wait_all(dp_copies)
+        base_group, tail_group = groups.new(), groups.new()
+        base_group.start(de_base.at[core, side], de_base.at[core, side], partner)
+        tail_group.start(de_tail.at[core, side], de_tail.at[core, side], partner)
+
+        def finish():
+            base_group.done(de_base.at[0, side])
+            tail_group.done(de_tail.at[0, side])
+
+        return finish
+
+    finish_pair = [send_de(0)]
+    finish_dp()
     de_base[core, 1] = gathered(dp_own_base, dp_land_base, row, rows)
     de_tail[core, 1] = gathered(dp_own_tail, dp_land_tail, row, rows)
-    pair_de += send_de(1)
-    wait_all(loss_copies)
+    finish_pair.append(send_de(1))
+    loss_group.done(loss_land.at[pl.ds(0, rows - 1)])
     loss = loss_land[0]
     for k in range(1, rows):
         loss = loss + loss_land[k]
     out_loss[...] = loss * (1.0 / (size * spare))
 
-    def keep(t, part, low):
-        high = low + part.shape[1]
+    low_count, high_count = 2, lanes // 2
+    low_lane, high_lane = lax.rem(lane, low_count), lax.div(lane, low_count)
+    low_others = [lax.rem(low_lane + k, low_count) for k in range(1, low_count)]
+    high_others = [lax.rem(high_lane + k, high_count) for k in range(1, high_count)]
+    skip, skip_two = half * lanes, half * high_count
+
+    def in_plane(high, low):
+        return plane * row + 2 * (high * low_count + low) + core
+
+    def first_stage(chunk_at, part):
+        t, cols = chunk_at
         for i in range(per_tile):
-            for m in range(lanes):
-                for j in range(2):
-                    at = ((i * lanes + m) * 2 + j) * chunk
-                    piece = part[at : at + chunk]
-                    own[t * per_tile + i, m, j, :, low:high] = piece
-                    outgoing[t * per_tile + i, m, j, :, low:high] = piece.astype(BF16)
-        made = []
-        block = pl.ds(t * per_tile, per_tile)
-        for k in range(1, lanes):
-            there = lax.rem(lane + k, lanes)
-            made.append(
-                copies.start(
-                    outgoing.at[block, there, :, :, pl.ds(low, high - low)],
-                    landing.at[lane, block, :, :, pl.ds(low, high - low)],
-                    plane * row + 2 * there + core,
-                )
+            for high in range(high_count):
+                for low in range(low_count):
+                    for j in range(2):
+                        at = (((i * high_count + high) * low_count + low) * 2 + j) * chunk
+                        piece = part[at : at + chunk]
+                        step = t * per_tile + i
+                        own[step, j, high, low, :, cols] = piece
+                        if j == 0:
+                            slot = (low * half + step) * high_count + high
+                        else:
+                            slot = skip + (high * half + step) * low_count + low
+                        outgoing[slot, :, cols] = piece.astype(BF16)
+        group = groups.new()
+        span = per_tile * high_count
+        for low in low_others:
+            group.start(
+                outgoing.at[pl.ds((low * half + t * per_tile) * high_count, span), :, cols],
+                landing.at[pl.ds((low_lane * half + t * per_tile) * high_count, span), :, cols],
+                in_plane(high_lane, low),
             )
-        return made
-
-    wait_all(pair_de)
-    de = jnp.concatenate([de_base[...].reshape(x_rows, embed), flat_rows(de_tail[...])], axis=0)
-    lane_copies = [keep(0, dot(all_hidden[0], de, 0, 0), width)]
-    for t in range(TILES):
-        start = pl.multiple_of(core * hidden_half + t * tile, 128)
-        back = dot(de, w_second[pl.ds(start, tile), :], 1, 1)
-        act_grad = (all_slope[t] * back).astype(BF16)
-        lane_copies[t] += keep(t, dot(act_grad, all_x[...], 0, 0), 0)
-        if t + 1 < TILES:
-            lane_copies.append(keep(t + 1, dot(all_hidden[t + 1], de, 0, 0), width))
-
-    sender_core = lax.div(row, half)
-
-    def line_copy(i, j):
+        span = per_tile * low_count
+        for high in high_others:
+            group.start(
+                outgoing.at[pl.ds(skip + (high * half + t * per_tile) * low_count, span), :, cols],
+                landing.at[pl.ds(skip + (high_lane * half + t * per_tile) * low_count, span), :, cols],
+                in_plane(high, low_lane),
+            )
+        return group
+
+    def second_stage(chunk_at, before):
+        t, cols = chunk_at
+        count = (low_count - 1) * high_count + (high_count - 1) * low_count
+        before.done(landing.at[pl.ds(0, per_tile * count), :, cols])
+        for i in range(t * per_tile, (t + 1) * per_tile):
+            for high in range(high_count):
+                total = own[i, 0, high, low_lane, :, cols]
+                for low in low_others:
+                    total = total + landing[(low * half + i) * high_count + high, :, cols].astype(F32)
+                own[i, 0, high, low_lane, :, cols] = total
+                outgoing_two[high * half + i, :, cols] = total.astype(BF16)
+            for low in range(low_count):
+                total = own[i, 1, high_lane, low, :, cols]
+                for high in high_others:
+                    slot = skip + (high * half + i) * low_count + low
+                    total = total + landing[slot, :, cols].astype(F32)
+                own[i, 1, high_lane, low, :, cols] = total
+                outgoing_two[skip_two + low * half + i, :, cols] = total.astype(BF16)
+        group = groups.new()
+        block = t * per_tile
+        for high in high_others:
+            group.start(
+                outgoing_two.at[pl.ds(high * half + block, per_tile), :, cols],
+                landing_two.at[pl.ds(high_lane * half + block, per_tile), :, cols],
+                in_plane(high, low_lane),
+            )
+        for low in low_others:
+            group.start(
+                outgoing_two.at[pl.ds(skip_two + low * half + block, per_tile), :, cols],
+                landing_two.at[pl.ds(skip_two + low_lane * half + block, per_tile), :, cols],
+                in_plane(high_lane, low),
+            )
+        return group
+
+    def line_copy(i, j, cols):
         return pltpu.make_async_remote_copy(
-            src_ref=forward.at[i, j],
-            dst_ref=landed.at[row],
+            src_ref=forward.at[i, j, :, cols],
+            dst_ref=landed.at[row, :, cols],
             send_sem=line_send.at[i, j],
             recv_sem=line_recv.at[row],
             device_id=(plane * (half * core + i) + column + j,),
             device_id_type=MESH,
         )
 
-    for t in range(TILES):
-        wait_all(lane_copies[t])
+    def third_stage(chunk_at, before):
+        t, cols = chunk_at
+        count = low_count - 1 + high_count - 1
+        before.done(landing_two.at[pl.ds(0, per_tile * count), :, cols])
         for i in range(t * per_tile, (t + 1) * per_tile):
             for j in range(2):
-                total = own[i, lane, j]
-                for k in range(1, lanes):
-                    total = total + landing[lax.rem(lane + k, lanes), i, j].astype(F32)
-                sums[i, j] = total
-                forward[i, j] = total.astype(BF16)
+                total = own[i, j, high_lane, low_lane, :, cols]
+                if j == 0:
+                    slots = [high * half + i for high in high_others]
+                else:
+                    slots = [skip_two + low * half + i for low in low_others]
+                for slot in slots:
+                    total = total + landing_two[slot, :, cols].astype(F32)
+                sums[i, j, :, cols] = total
+                forward[i, j, :, cols] = total.astype(BF16)
 
                 @pl.when(plane * (half * core + i) + column + j != me)
                 def _():
-                    line_copy(i, j).start()
-
+                    line_copy(i, j, cols).start()
+
+    for finish in finish_pair:
+        finish()
+    de = jnp.concatenate([de_base[...].reshape(x_rows, embed), flat_rows(de_tail[...])], axis=0)
+    act_grads = {}
+
+    def part_of(chunk_at):
+        t, cols = chunk_at
+        if cols.start >= width:
+            return dot(all_hidden[t], de[:, cols.start - width : cols.start - width + cols.size], 0, 0)
+        if t not in act_grads:
+            start = pl.multiple_of(core * hidden_half + t * tile, 128)
+            back = dot(de, w_second[pl.ds(start, tile), :], 1, 1)
+            act_grads[t] = (all_slope[t] * back).astype(BF16)
+        return dot(act_grads[t], all_x[:, cols], 0, 0)
+
+    piece = embed
+    chunks = []
+    for t in range(TILES):
+        chunks.append((t, pl.ds(width, piece)))
+        for low in range(0, width, piece):
+            chunks.append((t, pl.ds(low, piece)))
+    ones, twos = [], []
+    for at in range(len(chunks) + DELAY):
+        if at < len(chunks):
+            for ahead in range(len(ones), min(at + AHEAD, len(chunks))):
+                ones.append(first_stage(chunks[ahead], part_of(chunks[ahead])))
+            twos.append(second_stage(chunks[at], ones[at]))
+        if at >= DELAY:
+            third_stage(chunks[at - DELAY], twos[at - DELAY])
+
+    sender_core = lax.div(row, half)
+    whole = pl.ds(0, width + embed)
     for i in range(half):
         for j in range(2):
 
             @pl.when(plane * (half * core + i) + column + j != me)
             def _():
-                line_copy(i, j).wait_send()
+                line_copy(i, j, whole).wait_send()
 
     for sender_row in range(rows):
         sender = plane * sender_row + column + sender_core
@@ -508,8 +642,8 @@
     unit = base // 16
     block = base + unit
     vmem = pl.BlockSpec(memory_space=pltpu.VMEM)
-    count = 30 + 4 * (plane - 1) + 2 * (rows - 1) + 2
-    count += 2 * (plane - 1) + 3 * (rows - 1) + 4 + 2 * TILES * (lanes - 1)
+    anywhere = pl.BlockSpec(memory_space=pl.ANY)
+    count = 20 + 2 * TILES * (1 + width // embed)
 
     def split(members, dtype):
         return [
@@ -541,10 +675,13 @@
         pltpu.VMEM((rows, 8, 128), F32),
         pltpu.VMEM((2, 2, base, embed), BF16),
         pltpu.VMEM((2, 2, unit, embed), BF16),
+        pltpu.VMEM((2, unit, width), BF16),
         pltpu.VMEM((4 * block, width), BF16),
-        pltpu.VMEM((half, lanes, 2, chunk, across), F32),
-        pltpu.VMEM((half, lanes, 2, chunk, across), BF16),
-        pltpu.VMEM((lanes, half, 2, chunk, across), BF16),
+        pltpu.VMEM((half, 2, lanes // 2, 2, chunk, across), F32),
+        pltpu.VMEM((2 * half * lanes, chunk, across), BF16),
+        pltpu.VMEM((2 * half * lanes, chunk, across), BF16),
+        pltpu.VMEM((half * (lanes // 2 + 2), chunk, across), BF16),
+        pltpu.VMEM((half * (lanes // 2 + 2), chunk, across), BF16),
         pltpu.VMEM((half, 2, chunk, across), F32),
         pltpu.VMEM((half, 2, chunk, across), BF16),
         pltpu.VMEM((rows, chunk, across), BF16),
@@ -556,7 +693,7 @@
         pltpu.VMEM(w_second.shape, BF16),
         pltpu.VMEM((TILES, 4 * block, hidden_width // 2 // TILES), BF16),
         pltpu.VMEM((TILES, 4 * block, hidden_width // 2 // TILES), F32),
-        pltpu.SemaphoreType.DMA((2,)),
+        pltpu.SemaphoreType.DMA((8,)),
     ]
     return pl.pallas_call(
         functools.partial(step_kernel, size, plane, score_scale),
@@ -564,8 +701,8 @@
             jax.ShapeDtypeStruct((8, 128), F32),
             jax.ShapeDtypeStruct((chunk, across), F32),
         ],
-        in_specs=[pl.BlockSpec(memory_space=pltpu.SMEM)] + [vmem] * 3
-        + [pl.BlockSpec(memory_space=pl.ANY)] * 2,
+        in_specs=[pl.BlockSpec(memory_space=pltpu.SMEM)] + [anywhere] * 2 + [vmem]
+        + [anywhere] * 2,
         out_specs=[vmem] * 2,
         scratch_shapes=scratch,
         compiler_params=pltpu.CompilerParams(

time: 77.7 us -> 70.6 us (0.909)
  Pallas kernels: 76.9 us -> 69.8 us
    pallas_call x1, Pallas kernels: 75.2 us -> 68.1 us  [step(): pl.pallas_call(functools.partial(step_kernel, size, plane, score_scale),...]
where the time goes in v1:
time: 70.6 us; the launch traced here: 70.4 us
  Pallas kernels  69.8 us (99%)
    pallas_call x1, Pallas kernels, step(): pl.pallas_call(functools.partial(step_kernel, size, plane, score_scale),...  68.1 us
    pallas_call x1, Pallas kernels, split_outputs(): pl.pallas_call(split_kernel, out_shape=[jax.ShapeDtypeStruct((1,), F32),...  1.65 us

profile of v1, /device:TPU:9, one launch (start us, length us, event | category | flops | bytes accessed | tf_op | source)
XLA Modules:
  0.0 70.4 jit_solution(9436514414407618384)
XLA Ops:
  0.6 68.1 %shard_map.85 = (f32[8,128]{1,0:T(8,128)}, f32[48,1152]{1,0:T(8,128)}) custom-call(s32[32]{0:T(128)} %counts.1, bf16[256,768]{1,0:T(8,128)(2,1)} %query_hbm.1, bf16[256,768]{1,0:T(8,128)(2,1)} %passage_hbm.1, s32[1,256]{1,0:T(1,128)} %bitcast.3, bf16[768,1536]{1,0:T(8,128)(2,1)} %w_first_hbm.1, bf16[1536,384]{1,0:T(8,128)(2,1)} %w_second_hbm.1), custom_call_target="tpu_custom_call" | custom-call | tf_op jit(solution)/shard_map/pallas_call | solution.py:698
  68.8 1.6 %shard_map.86 = (f32[1]{0:T(128)}, f32[48,768]{1,0:T(8,128)}, f32[48,384]{1,0:T(8,128)}) custom-call(f32[8,128]{1,0:T(8,128)} %get-tuple-element.8.loss, f32[48,1152]{1,0:T(8,128)} %get-tuple-element.9.total), custom_call_target="tpu_custom_call" | custom-call | tf_op jit(solution)/shard_map/pallas_call | solution.py:621

commit v2 on v1

--- a/solution.py
+++ b/solution.py
@@ -93,12 +93,15 @@
     q_base,
     q_tail,
     p_base,
-    p_tail,
+    q_unit,
+    q_unit_land,
+    p_tails,
     pos_land,
     all_q,
     all_p,
     scores,
     stat_land,
+    found_land,
     dq_own_base,
     dq_own_tail,
     dq_out_base,
@@ -114,7 +117,6 @@
     loss_land,
     de_base,
     de_tail,
-    own_tail,
     all_x,
     own,
     outgoing,
@@ -158,6 +160,14 @@
 
     plane_peers = [row * plane + lax.rem(spot + k, plane) for k in range(1, plane)]
     line_peers = [lax.rem(row + k, rows) * plane + spot for k in range(1, rows)]
+    bits = [1 << at for at in range(lanes.bit_length() - 1)]
+    lane_others = []
+    for flips in range(1, lanes):
+        away = lane
+        for bit in bits:
+            if flips & bit:
+                away = away + bit - 2 * bit * lax.rem(lax.div(lane, bit), 2)
+        lane_others.append(away)
     barrier = pltpu.get_barrier_semaphore()
 
     def greet(device):
@@ -184,6 +194,9 @@
                 units.at[lax.div(there, near), lax.rem(there, near), :, side],
                 load_sems.at[sem],
             ).start()
+        pltpu.make_async_copy(
+            features.at[pl.ds(base, unit), :], units.at[row, aside, :, side], load_sems.at[sem]
+        ).start()
     base_loads = [
         pltpu.make_async_copy(
             features.at[pl.ds(0, base), :], feat_base.at[core, at], load_sems.at[2 + at]
@@ -194,19 +207,13 @@
         pltpu.make_async_copy(w_first_hbm, w_first, load_sems.at[4]),
         pltpu.make_async_copy(w_second_hbm, w_second, load_sems.at[5]),
     ]
-    tail_loads = [
-        pltpu.make_async_copy(
-            features.at[pl.ds(base, unit), :], own_tail.at[at], load_sems.at[6 + at]
-        )
-        for at, features in enumerate((query_hbm, passage_hbm))
-    ]
-    for load in base_loads + weight_loads + tail_loads:
+    for load in base_loads + weight_loads:
         load.start()
     unit_pos[place] = positives[...].astype(F32)
 
     pl.semaphore_wait(barrier, 15 + plane - 1 + 2 * rows - 1)
     for features, sem in ((query_hbm, 0), (passage_hbm, 1)):
-        extra = features.at[pl.ds(spare, 15 * unit), :]
+        extra = features.at[pl.ds(base, 16 * unit), :]
         pltpu.make_async_copy(extra, extra, load_sems.at[sem]).wait()
 
     mid_group = groups.new()
@@ -260,103 +267,182 @@
     pair_base.start(feat_base.at[core], feat_base.at[core], partner)
     for load in weight_loads:
         load.wait()
-    embedded = tower(feat_base[core].reshape(2 * base, width))
-    q_base[spot] = embedded[:base]
-    p_base[row] = embedded[base:]
-    q_group, p_group = groups.new(), groups.new()
-    for device in plane_peers:
-        q_group.start(q_base.at[spot], q_base.at[spot], device)
+    p_base[row] = tower(feat_base[core, 1])
+    p_groups = [groups.new() for _ in range(rows)]
+    relayed = rows == 4
+    if relayed:
+
+        def p_send(block, there, group):
+            group.start(p_base.at[block], p_base.at[block], there * plane + spot)
+
+        for at, order in enumerate(((2, 1), (3, 2, 0), (0, 1, 3), (1, 2))):
+
+            @pl.when(row == at)
+            def _():
+                for there in order:
+                    p_send(at, there, p_groups[at])
+    else:
+        for k in range(1, rows):
+            p_groups[k].start(p_base.at[row], p_base.at[row], line_peers[k - 1])
+    q_base[spot] = tower(feat_base[core, 0])
+    q_pair = groups.new()
+    q_pair.start(q_base.at[spot], q_base.at[spot], partner)
+    q_groups = []
+    for away in lane_others:
+        group = groups.new()
+        group.start(q_base.at[spot], q_base.at[spot], row * plane + 2 * away + core)
+        q_groups.append(group)
+
     mid_group.done(unit_mid.at[pl.ds(0, near - 1)])
     source_row, source_aside = jnp.int32(0), heavy_place
     for k in range(1, rows):
         beyond = heavy_place >= k * near
         source_row = source_row + jnp.where(beyond, 1, 0)
         source_aside = source_aside - jnp.where(beyond, near, 0)
-    unit_pass[...] = jnp.where(source_aside == aside, units[:, aside], unit_mid[source_aside])
-    pass_group = groups.new()
+    passed = jnp.where(
+        source_aside == aside, units[:, aside].astype(F32), unit_mid[source_aside].astype(F32)
+    )
+    unit_pass[...] = passed.astype(BF16)
+    tails = rows * unit
+    mid_x = jnp.concatenate(
+        [passed[:, :, :width].reshape(tails, width), passed[:, :, width:].reshape(tails, width)],
+        axis=0,
+    ).astype(BF16)
+    mid_e = tower(mid_x)
+    q_unit[...] = mid_e[:tails].astype(F32).reshape(rows, unit, embed).astype(BF16)
+    p_tails[row] = mid_e[tails:]
+    q_unit_group, p_tail_group, pass_group = groups.new(), groups.new(), groups.new()
     for k in range(1, rows):
         there = lax.rem(row + k, rows)
-        pass_group.start(unit_pass.at[there], unit_land.at[row], there * plane + spot)
+        q_unit_group.start(q_unit.at[there], q_unit_land.at[row], there * plane + spot)
     for device in line_peers:
-        p_group.start(p_base.at[row], p_base.at[row], device)
+        p_tail_group.start(p_tails.at[row], p_tails.at[row], device)
 
     where_group.done(unit_pos.at[pl.ds(0, 15)])
-    pass_group.done(unit_land.at[pl.ds(0, rows - 1)])
-    for load in tail_loads:
-        load.wait()
-    heavy = source == me
-    got = jnp.where(source_row == row, unit_pass[row], unit_land[source_row]).astype(F32)
-    tail_q = jnp.where(heavy, own_tail[0].astype(F32), got[:, :width])
-    tail_p = jnp.where(heavy, own_tail[1].astype(F32), got[:, width:])
     slots = lax.broadcasted_iota(jnp.int32, (unit, positives.shape[1]), 1)
     chosen = lax.broadcasted_iota(jnp.int32, slots.shape, 0) + tail_row(me)
     tail_pos = jnp.sum(
         jnp.where(slots == chosen, unit_pos[heavy_place], 0.0), axis=1, keepdims=True
     )
-    tail_x = jnp.concatenate([tail_q, tail_p], axis=0)
-    feat_tail[core] = tail_x.reshape(2, unit, width).astype(BF16)
-    tail_e = tower(tail_x.astype(BF16)).astype(F32)
-    q_tail[spot] = tail_e[:unit].astype(BF16)
-    p_tail[row] = tail_e[unit:].astype(BF16)
     pos_land[spot, 0] = positives[:, :base].astype(F32)
     sub = lax.broadcasted_iota(jnp.int32, (unit, base), 0) + spot * unit
     along = lax.broadcasted_iota(jnp.int32, (unit, base), 1)
     pos_land[spot, 1] = jnp.sum(jnp.where(sub == along, tail_pos, 0.0), axis=0, keepdims=True)
-    q_tail_group, p_tail_group, pos_group = groups.new(), groups.new(), groups.new()
+    pos_group = groups.new()
     for device in plane_peers:
         pos_group.start(pos_land.at[spot], pos_land.at[spot], device)
+
+    if relayed:
+        for at, (far, end) in ((1, (3, 0)), (2, (0, 3))):
+
+            @pl.when(row == at)
+            def _():
+                p_groups[far].landed(p_base.at[far])
+                p_send(far, end, p_groups[far])
+
+    q_unit_group.done(q_unit_land.at[pl.ds(0, rows - 1)])
+    q_tail[spot] = jnp.where(
+        source_row == row, q_unit[row].astype(F32), q_unit_land[source_row].astype(F32)
+    ).astype(BF16)
+    q_tail_group = groups.new()
+    for device in plane_peers:
         q_tail_group.start(q_tail.at[spot], q_tail.at[spot], device)
-    for device in line_peers:
-        p_tail_group.start(p_tail.at[row], p_tail.at[row], device)
-    pair_tail = groups.new()
-    pair_tail.start(feat_tail.at[core], feat_tail.at[core], partner)
-    q_group.done(q_base.at[pl.ds(0, plane - 1)])
-    q_tail_group.done(q_tail.at[pl.ds(0, plane - 1)])
-    pos_group.done(pos_land.at[pl.ds(0, plane - 1)])
-    p_group.done(p_base.at[pl.ds(0, rows - 1)])
-    p_tail_group.done(p_tail.at[pl.ds(0, rows - 1)])
+    for k in range(1, rows):
+        there = lax.rem(row + k, rows)
+        pass_group.start(unit_pass.at[there], unit_land.at[row], there * plane + spot)
+
+    for away, group in zip(lane_others, q_groups):
+        there = 2 * away + core
+        group.done(q_base.at[there])
+        q_pair.start(q_base.at[there], q_base.at[there], partner)
+    if relayed:
+        for at in range(rows):
+            early = {0: 2, 3: 1}.get(at, at)
+
+            @pl.when(jnp.logical_and(row != at, row != early))
+            def _():
+                p_groups[at].landed(p_base.at[at])
+    else:
+        for k in range(1, rows):
+            p_groups[k].done(p_base.at[lax.rem(row + rows - k, rows)])
+    q_pair.done(q_base.at[pl.ds(0, lanes)])
 
     q_rows, p_rows = plane * base, rows * base
-    all_q[:q_rows] = q_base[...].reshape(q_rows, embed)
-    all_q[q_rows:] = flat_rows(q_tail[...])
-    all_p[:p_rows] = p_base[...].reshape(p_rows, embed)
-    all_p[p_rows:] = flat_rows(p_tail[...])
-    pos_tail = pos_land[0, 1]
-    for k in range(1, plane):
-        pos_tail = pos_tail + pos_land[k, 1]
-    wanted = jnp.concatenate(
-        [pos_land[k, 0] for k in range(plane)] + [pos_tail[:, : plane * unit]], axis=1
-    )
     line = [plane * k + spot for k in range(rows)]
-    ids = jnp.concatenate(
-        [lax.broadcasted_iota(jnp.int32, (base, 1), 0) + offset_of(device) for device in line]
-        + [
+    base_ids = jnp.concatenate(
+        [lax.broadcasted_iota(jnp.int32, (base, 1), 0) + offset_of(device) for device in line],
+        axis=0,
+    ).astype(F32)
+    tail_ids = jnp.concatenate(
+        [
             lax.broadcasted_iota(jnp.int32, (unit, 1), 0) + offset_of(source) + tail_row(device)
             for device in line
         ],
         axis=0,
     ).astype(F32)
-    scores[...] = score_scale * dot(all_p[...], all_q[...], 1, 1)
-    value = scores[...]
+    all_q[:q_rows] = q_base[...].reshape(q_rows, embed)
+    all_p[:p_rows] = p_base[...].reshape(p_rows, embed)
+    pos_group.done(pos_land.at[pl.ds(0, plane - 1)])
+    base_wanted = jnp.concatenate([pos_land[k, 0] for k in range(plane)], axis=1)
+
+    def spread(value, ids, wanted):
+        top = jnp.max(value, axis=0, keepdims=True)
+        mass = jnp.sum(jnp.exp(value - top), axis=0, keepdims=True)
+        return top, mass, jnp.sum(jnp.where(ids == wanted, value, 0.0), axis=0, keepdims=True)
+
+    def merge(one, two):
+        top = jnp.maximum(one[0], two[0])
+        mass = one[1] * jnp.exp(one[0] - top) + two[1] * jnp.exp(two[0] - top)
+        return top, mass, one[2] + two[2]
+
+    def scored(p_part, q_part):
+        scores[p_part, q_part] = score_scale * dot(all_p[p_part], all_q[q_part], 1, 1)
+        return scores[p_part, q_part]
+
+    p_base_part, p_tail_part = slice(0, p_rows), slice(p_rows, all_p.shape[0])
+    q_base_part, q_tail_part = slice(0, q_rows), slice(q_rows, all_q.shape[0])
+    base_stats = spread(scored(p_base_part, q_base_part), base_ids, base_wanted)
+
+    p_tail_group.done(p_tails.at[pl.ds(0, rows - 1)])
+    all_p[p_rows:] = p_tails[source_row]
+    base_stats = merge(
+        base_stats, spread(scored(p_tail_part, q_base_part), tail_ids, base_wanted)
+    )
+    q_tail_group.done(q_tail.at[pl.ds(0, plane - 1)])
+    all_q[q_rows:] = flat_rows(q_tail[...])
+    pos_tail = pos_land[0, 1]
+    for k in range(1, plane):
+        pos_tail = pos_tail + pos_land[k, 1]
+    tail_wanted = pos_tail[:, : plane * unit]
+    ids = jnp.concatenate([base_ids, tail_ids], axis=0)
+    tail_stats = spread(scored(slice(0, all_p.shape[0]), q_tail_part), ids, tail_wanted)
+    stat_land[spot, 0:1, :q_rows] = base_stats[0]
+    stat_land[spot, 0:1, q_rows:] = tail_stats[0]
+    stat_land[spot, 1:2, :q_rows] = base_stats[1]
+    stat_land[spot, 1:2, q_rows:] = tail_stats[1]
+    found_land[spot, :, :q_rows] = base_stats[2]
+    found_land[spot, :, q_rows:] = tail_stats[2]
+    wanted = jnp.concatenate([base_wanted, tail_wanted], axis=1)
     hit = ids == wanted
-    top = jnp.max(value, axis=0, keepdims=True)
-    stat_land[spot, 0:1] = top
-    stat_land[spot, 1:2] = jnp.sum(jnp.exp(value - top), axis=0, keepdims=True)
-    stat_land[spot, 2:3] = jnp.sum(jnp.where(hit, value, 0.0), axis=0, keepdims=True)
-    stat_land[spot, 3:4] = jnp.zeros_like(top)
-    stat_group = groups.new()
+    stat_group, found_group = groups.new(), groups.new()
     for device in plane_peers:
         stat_group.start(stat_land.at[spot], stat_land.at[spot], device)
+    for device in plane_peers:
+        found_group.start(found_land.at[spot], found_land.at[spot], device)
+    pass_group.done(unit_land.at[pl.ds(0, rows - 1)])
+    got = jnp.where(
+        source_row == row, unit_pass[row].astype(F32), unit_land[source_row].astype(F32)
+    )
+    feat_tail[core, 0] = got[:, :width].astype(BF16)
+    feat_tail[core, 1] = got[:, width:].astype(BF16)
+    pair_tail = groups.new()
+    pair_tail.start(feat_tail.at[core], feat_tail.at[core], partner)
     stat_group.done(stat_land.at[pl.ds(0, plane - 1)])
     stats = stat_land[...]
     tops = stats[:, 0]
     row_top = jnp.max(tops, axis=0, keepdims=True)
     mass = jnp.sum(stats[:, 1] * jnp.exp(tops - row_top), axis=0, keepdims=True)
     log_norm = row_top + jnp.log(mass)
-    found = jnp.sum(stats[:, 2], axis=0, keepdims=True)
-    loss_land[row] = jnp.broadcast_to(
-        jnp.sum(log_norm - found, axis=1, keepdims=True), loss_land.shape[1:]
-    )
     grads_t = (jnp.exp(scores[...] - log_norm) - hit.astype(F32)).astype(BF16)
 
     def scatter(part, own_base, own_tail, out_base, out_tail, land_base, land_tail, mine, peers):
@@ -403,6 +489,11 @@
         dp_land_tail,
         row,
         [(lax.rem(row + k, rows), line_peers[k - 1]) for k in range(1, rows)],
+    )
+    found_group.done(found_land.at[pl.ds(0, plane - 1)])
+    found = jnp.sum(found_land[...][:, 0], axis=0, keepdims=True)
+    loss_land[row] = jnp.broadcast_to(
+        jnp.sum(log_norm - found, axis=1, keepdims=True), loss_land.shape[1:]
     )
     loss_group = groups.new()
     for device in line_peers:
@@ -578,6 +669,16 @@
         if at >= DELAY:
             third_stage(chunks[at - DELAY], twos[at - DELAY])
 
+    if relayed:
+        for at in range(rows):
+
+            @pl.when(row == at)
+            def _():
+                p_groups[at].sent(p_base.at[pl.ds(0, 3 if at in (1, 2) else 2)])
+                if at in (1, 2):
+                    far = 3 if at == 1 else 0
+                    p_groups[far].sent(p_base.at[far])
+
     sender_core = lax.div(row, half)
     whole = pl.ds(0, width + embed)
     for i in range(half):
@@ -643,7 +744,7 @@
     block = base + unit
     vmem = pl.BlockSpec(memory_space=pltpu.VMEM)
     anywhere = pl.BlockSpec(memory_space=pl.ANY)
-    count = 20 + 2 * TILES * (1 + width // embed)
+    count = 20 + rows + lanes + 2 * TILES * (1 + width // embed)
 
     def split(members, dtype):
         return [
@@ -660,12 +761,16 @@
         pltpu.VMEM((2, 2, base, width), BF16),
         pltpu.VMEM((2, 2, unit, width), BF16),
         *split(plane, BF16),
-        *split(rows, BF16),
+        pltpu.VMEM((rows, base, embed), BF16),
+        pltpu.VMEM((rows, unit, embed), BF16),
+        pltpu.VMEM((rows, unit, embed), BF16),
+        pltpu.VMEM((rows, rows * unit, embed), BF16),
         pltpu.VMEM((plane, 2, 1, base), F32),
         pltpu.VMEM((plane * block, embed), BF16),
         pltpu.VMEM((rows * block, embed), BF16),
         pltpu.VMEM((rows * block, plane * block), F32),
-        pltpu.VMEM((plane, 4, plane * block), F32),
+        pltpu.VMEM((plane, 2, plane * block), F32),
+        pltpu.VMEM((plane, 1, plane * block), F32),
         *split(plane, F32),
         *split(plane, BF16),
         *split(plane, BF16),
@@ -675,7 +780,6 @@
         pltpu.VMEM((rows, 8, 128), F32),
         pltpu.VMEM((2, 2, base, embed), BF16),
         pltpu.VMEM((2, 2, unit, embed), BF16),
-        pltpu.VMEM((2, unit, width), BF16),
         pltpu.VMEM((4 * block, width), BF16),
         pltpu.VMEM((half, 2, lanes // 2, 2, chunk, across), F32),
         pltpu.VMEM((2 * half * lanes, chunk, across), BF16),
@@ -693,7 +797,7 @@
         pltpu.VMEM(w_second.shape, BF16),
         pltpu.VMEM((TILES, 4 * block, hidden_width // 2 // TILES), BF16),
         pltpu.VMEM((TILES, 4 * block, hidden_width // 2 // TILES), F32),
-        pltpu.SemaphoreType.DMA((8,)),
+        pltpu.SemaphoreType.DMA((6,)),
     ]
     return pl.pallas_call(
         functools.partial(step_kernel, size, plane, score_scale),

time: 70.6 us -> 64.3 us (0.911)
  Pallas kernels: 69.8 us -> 63.4 us
    pallas_call x1, Pallas kernels: 68.1 us -> 61.8 us  [step(): pl.pallas_call(functools.partial(step_kernel, size, plane, score_scale),...]
where the time goes in v2:
time: 64.3 us; the launch traced here: 64 us
  Pallas kernels  63.4 us (99%)
    pallas_call x1, Pallas kernels, step(): pl.pallas_call(functools.partial(step_kernel, size, plane, score_scale),...  61.8 us
    pallas_call x1, Pallas kernels, split_outputs(): pl.pallas_call(split_kernel, out_shape=[jax.ShapeDtypeStruct((1,), F32),...  1.65 us

profile of v2, /device:TPU:9, one launch (start us, length us, event | category | flops | bytes accessed | tf_op | source)
XLA Modules:
  0.0 64.0 jit_solution(990890945573063001)
XLA Ops:
  0.6 61.8 %shard_map.85 = (f32[8,128]{1,0:T(8,128)}, f32[48,1152]{1,0:T(8,128)}) custom-call(s32[32]{0:T(128)} %counts.1, bf16[256,768]{1,0:T(8,128)(2,1)} %query_hbm.1, bf16[256,768]{1,0:T(8,128)(2,1)} %passage_hbm.1, s32[1,256]{1,0:T(1,128)} %bitcast.3, bf16[768,1536]{1,0:T(8,128)(2,1)} %w_first_hbm.1, bf16[1536,384]{1,0:T(8,128)(2,1)} %w_second_hbm.1), custom_call_target="tpu_custom_call" | custom-call | tf_op jit(solution)/shard_map/pallas_call | solution.py:802
  62.4 1.6 %shard_map.86 = (f32[1]{0:T(128)}, f32[48,768]{1,0:T(8,128)}, f32[48,384]{1,0:T(8,128)}) custom-call(f32[8,128]{1,0:T(8,128)} %get-tuple-element.8.loss, f32[48,1152]{1,0:T(8,128)} %get-tuple-element.9.total), custom_call_target="tpu_custom_call" | custom-call | tf_op jit(solution)/shard_map/pallas_call | solution.py:722

commit v3 on v2

--- a/solution.py
+++ b/solution.py
@@ -68,6 +68,7 @@
 
     def new(self):
         self.used += 1
+        assert self.used <= self.send.shape[0]
         return Group(self.send.at[self.used - 1], self.recv.at[self.used - 1])
 
 
@@ -83,16 +84,20 @@
     w_second_hbm,
     out_loss,
     out_all,
-    units,
-    unit_mid,
+    units_q,
+    units_p,
+    unit_mid_q,
+    unit_mid_p,
     unit_pass,
     unit_land,
     unit_pos,
     feat_base,
     feat_tail,
     q_base,
+    p_base,
     q_tail,
-    p_base,
+    q_extra,
+    q_mid,
     q_unit,
     q_unit_land,
     p_tails,
@@ -104,6 +109,8 @@
     found_land,
     dq_own_base,
     dq_own_tail,
+    dq_pair_base,
+    dq_pair_tail,
     dq_out_base,
     dq_out_tail,
     dq_land_base,
@@ -114,6 +121,8 @@
     dp_out_tail,
     dp_land_base,
     dp_land_tail,
+    dp_relay_base,
+    dp_relay_tail,
     loss_land,
     de_base,
     de_tail,
@@ -151,7 +160,7 @@
     width, hidden_width = w_first.shape
     embed = w_second.shape[1]
     base = q_base.shape[1]
-    unit = q_tail.shape[1]
+    unit = unit_pass.shape[1]
     hidden_half = hidden_width // 2
     tile = hidden_half // TILES
     per_tile = half // TILES
@@ -185,17 +194,16 @@
     spare = base + unit
     near = plane // stride
     aside = lax.div(spot, stride)
-    for at, (features, sem) in enumerate(((query_hbm, 0), (passage_hbm, 1))):
-        side = pl.ds(at * width, width)
+    for features, units, sem in ((passage_hbm, units_p, 1), (query_hbm, units_q, 0)):
         for u in range(15):
             there = u + lax.div(u + 16 - place, 16)
             pltpu.make_async_copy(
                 features.at[pl.ds(spare + u * unit, unit), :],
-                units.at[lax.div(there, near), lax.rem(there, near), :, side],
+                units.at[lax.div(there, near), lax.rem(there, near)],
                 load_sems.at[sem],
             ).start()
         pltpu.make_async_copy(
-            features.at[pl.ds(base, unit), :], units.at[row, aside, :, side], load_sems.at[sem]
+            features.at[pl.ds(base, unit), :], units.at[row, aside], load_sems.at[sem]
         ).start()
     base_loads = [
         pltpu.make_async_copy(
@@ -212,18 +220,24 @@
     unit_pos[place] = positives[...].astype(F32)
 
     pl.semaphore_wait(barrier, 15 + plane - 1 + 2 * rows - 1)
-    for features, sem in ((query_hbm, 0), (passage_hbm, 1)):
+
+    def units_loaded(features, sem):
         extra = features.at[pl.ds(base, 16 * unit), :]
         pltpu.make_async_copy(extra, extra, load_sems.at[sem]).wait()
 
-    mid_group = groups.new()
-    for k in range(1, near):
-        there = lax.rem(aside + k, near)
-        mid_group.start(
-            units.at[:, there],
-            unit_mid.at[aside],
-            row * plane + there * stride + lax.rem(me, stride),
-        )
+    def spread_units(units, unit_mid):
+        group = groups.new()
+        for k in range(1, near):
+            there = lax.rem(aside + k, near)
+            group.start(
+                units.at[:, there],
+                unit_mid.at[aside],
+                row * plane + there * stride + lax.rem(me, stride),
+            )
+        return group
+
+    units_loaded(passage_hbm, 1)
+    mid_p_group = spread_units(units_p, unit_mid_p)
     where_group = groups.new()
     for k in range(1, 16):
         device = lax.rem(place + k, 16) * stride + lax.rem(me, stride)
@@ -238,9 +252,23 @@
     source = jnp.int32(0)
     for g in range(stride):
         source = source + jnp.where(lax.rem(me, stride) == g, heavies[g], 0)
-    heavy_place = jnp.int32(0)
-    for k in range(16):
-        heavy_place = heavy_place + jnp.where(source >= stride * (k + 1), 1, 0)
+
+    def place_of(device):
+        found_place = jnp.int32(0)
+        for k in range(16):
+            found_place = found_place + jnp.where(device >= stride * (k + 1), 1, 0)
+        return found_place
+
+    def row_and_aside(at):
+        found_row, found_aside = jnp.int32(0), at
+        for k in range(1, rows):
+            beyond = at >= k * near
+            found_row = found_row + jnp.where(beyond, 1, 0)
+            found_aside = found_aside - jnp.where(beyond, near, 0)
+        return found_row, found_aside
+
+    heavy_place = place_of(source)
+    source_row, source_aside = row_and_aside(heavy_place)
 
     def offset_of(device):
         before = jnp.int32(0)
@@ -267,7 +295,12 @@
     pair_base.start(feat_base.at[core], feat_base.at[core], partner)
     for load in weight_loads:
         load.wait()
-    p_base[row] = tower(feat_base[core, 1])
+    units_loaded(query_hbm, 0)
+    extra_x = flat_rows(units_q[...].reshape(16, unit, width))
+    first_e = tower(jnp.concatenate([feat_base[core, 1], extra_x], axis=0))
+    q_extra[...] = first_e[base:].astype(F32).reshape(q_extra.shape).astype(BF16)
+    mid_e_group = spread_units(q_extra, q_mid)
+    p_base[row] = first_e[:base]
     p_groups = [groups.new() for _ in range(rows)]
     relayed = rows == 4
     if relayed:
@@ -292,29 +325,25 @@
         group = groups.new()
         group.start(q_base.at[spot], q_base.at[spot], row * plane + 2 * away + core)
         q_groups.append(group)
-
-    mid_group.done(unit_mid.at[pl.ds(0, near - 1)])
-    source_row, source_aside = jnp.int32(0), heavy_place
-    for k in range(1, rows):
-        beyond = heavy_place >= k * near
-        source_row = source_row + jnp.where(beyond, 1, 0)
-        source_aside = source_aside - jnp.where(beyond, near, 0)
-    passed = jnp.where(
-        source_aside == aside, units[:, aside].astype(F32), unit_mid[source_aside].astype(F32)
-    )
-    unit_pass[...] = passed.astype(BF16)
-    tails = rows * unit
-    mid_x = jnp.concatenate(
-        [passed[:, :, :width].reshape(tails, width), passed[:, :, width:].reshape(tails, width)],
-        axis=0,
-    ).astype(BF16)
-    mid_e = tower(mid_x)
-    q_unit[...] = mid_e[:tails].astype(F32).reshape(rows, unit, embed).astype(BF16)
-    p_tails[row] = mid_e[tails:]
-    q_unit_group, p_tail_group, pass_group = groups.new(), groups.new(), groups.new()
+    mid_q_group = spread_units(units_q, unit_mid_q)
+
+    def picked(units, unit_mid):
+        return jnp.where(
+            source_aside == aside, units[:, aside].astype(F32), unit_mid[source_aside].astype(F32)
+        )
+
+    mid_e_group.done(q_mid.at[pl.ds(0, near - 1)])
+    q_unit[...] = picked(q_extra, q_mid).astype(BF16)
+    q_unit_group = groups.new()
     for k in range(1, rows):
         there = lax.rem(row + k, rows)
         q_unit_group.start(q_unit.at[there], q_unit_land.at[row], there * plane + spot)
+    mid_p_group.done(unit_mid_p.at[pl.ds(0, near - 1)])
+    passed = picked(units_p, unit_mid_p)
+    unit_pass[:, :, width:] = passed.astype(BF16)
+    tails = rows * unit
+    p_tails[row] = tower(passed.reshape(tails, width).astype(BF16))
+    p_tail_group, pass_group = groups.new(), groups.new()
     for device in line_peers:
         p_tail_group.start(p_tails.at[row], p_tails.at[row], device)
 
@@ -340,6 +369,13 @@
                 p_groups[far].landed(p_base.at[far])
                 p_send(far, end, p_groups[far])
 
+    def forward_q(at):
+        there = 2 * lane_others[at] + core
+        q_groups[at].done(q_base.at[there])
+        q_pair.start(q_base.at[there], q_base.at[there], partner)
+
+    for at in range(lanes - 1):
+        forward_q(at)
     q_unit_group.done(q_unit_land.at[pl.ds(0, rows - 1)])
     q_tail[spot] = jnp.where(
         source_row == row, q_unit[row].astype(F32), q_unit_land[source_row].astype(F32)
@@ -347,14 +383,6 @@
     q_tail_group = groups.new()
     for device in plane_peers:
         q_tail_group.start(q_tail.at[spot], q_tail.at[spot], device)
-    for k in range(1, rows):
-        there = lax.rem(row + k, rows)
-        pass_group.start(unit_pass.at[there], unit_land.at[row], there * plane + spot)
-
-    for away, group in zip(lane_others, q_groups):
-        there = 2 * away + core
-        group.done(q_base.at[there])
-        q_pair.start(q_base.at[there], q_base.at[there], partner)
     if relayed:
         for at in range(rows):
             early = {0: 2, 3: 1}.get(at, at)
@@ -403,6 +431,11 @@
     q_base_part, q_tail_part = slice(0, q_rows), slice(q_rows, all_q.shape[0])
     base_stats = spread(scored(p_base_part, q_base_part), base_ids, base_wanted)
 
+    mid_q_group.done(unit_mid_q.at[pl.ds(0, near - 1)])
+    unit_pass[:, :, :width] = picked(units_q, unit_mid_q).astype(BF16)
+    for k in range(1, rows):
+        there = lax.rem(row + k, rows)
+        pass_group.start(unit_pass.at[there], unit_land.at[row], there * plane + spot)
     p_tail_group.done(p_tails.at[pl.ds(0, rows - 1)])
     all_p[p_rows:] = p_tails[source_row]
     base_stats = merge(
@@ -445,51 +478,46 @@
     log_norm = row_top + jnp.log(mass)
     grads_t = (jnp.exp(scores[...] - log_norm) - hit.astype(F32)).astype(BF16)
 
-    def scatter(part, own_base, own_tail, out_base, out_tail, land_base, land_tail, mine, peers):
-        split = own_base.shape[0] * base
-        own_base[...] = part[:split].reshape(own_base.shape)
-        own_tail[...] = part[split:].reshape(own_tail.shape)
-        out_base[...] = own_base[...].astype(out_base.dtype)
-        out_tail[...] = own_tail[...].astype(out_tail.dtype)
-        base_group, tail_group = groups.new(), groups.new()
-        for there, device in peers:
-            base_group.start(out_base.at[there], land_base.at[mine], device)
-            tail_group.start(out_tail.at[there], land_tail.at[mine], device)
-
-        def finish():
-            base_group.done(land_base.at[pl.ds(0, len(peers))])
-            tail_group.done(land_tail.at[pl.ds(0, len(peers))])
-
-        return finish
-
-    def gathered(own_part, land, mine, members):
-        total = own_part[mine]
-        for k in range(1, members):
-            total = total + land[lax.rem(mine + k, members)].astype(F32)
-        return total.astype(BF16)
-
-    finish_dq = scatter(
-        score_scale * dot(grads_t, all_p[...], 0, 0),
-        dq_own_base,
-        dq_own_tail,
-        dq_out_base,
-        dq_out_tail,
-        dq_land_base,
-        dq_land_tail,
-        spot,
-        [(lax.rem(spot + k, plane), plane_peers[k - 1]) for k in range(1, plane)],
-    )
-    finish_dp = scatter(
-        score_scale * dot(grads_t, all_q[...], 1, 0),
-        dp_own_base,
-        dp_own_tail,
-        dp_out_base,
-        dp_out_tail,
-        dp_land_base,
-        dp_land_tail,
-        row,
-        [(lax.rem(row + k, rows), line_peers[k - 1]) for k in range(1, rows)],
-    )
+    def hold(part, own_base, own_tail):
+        rows_here = own_base.shape[0] * base
+        own_base[...] = part[:rows_here].reshape(own_base.shape)
+        own_tail[...] = part[rows_here:].reshape(own_tail.shape)
+
+    dp_group, dp_tail_group, relay_group, relay_tail_group = [groups.new() for _ in range(4)]
+
+    def send_dp(block, there, mine):
+        device = there * plane + spot
+        dp_group.start(dp_out_base.at[block], dp_land_base.at[mine], device)
+        dp_tail_group.start(dp_out_tail.at[block], dp_land_tail.at[mine], device)
+
+    hold(score_scale * dot(grads_t, all_q[...], 1, 0), dp_own_base, dp_own_tail)
+    dp_out_base[...] = dp_own_base[...].astype(BF16)
+    dp_out_tail[...] = dp_own_tail[...].astype(BF16)
+    if relayed:
+        for at, far, near_row, order in (
+            (0, 3, 1, (2, 1)), (1, None, None, (2, 0)), (2, None, None, (1, 3)), (3, 0, 2, (1, 2))
+        ):
+
+            @pl.when(row == at)
+            def _():
+                if far is not None:
+                    device = near_row * plane + spot
+                    relay_group.start(dp_out_base.at[far], dp_relay_base, device)
+                    relay_tail_group.start(dp_out_tail.at[far], dp_relay_tail, device)
+                for there in order:
+                    send_dp(there, there, at)
+    else:
+        for k in range(1, rows):
+            there = lax.rem(row + k, rows)
+            send_dp(there, there, row)
+
+    hold(score_scale * dot(grads_t, all_p[...], 0, 0), dq_own_base, dq_own_tail)
+    all_lanes = lane_others + [lane]
+    pair_groups, pair_tail_group = [groups.new() for _ in all_lanes], groups.new()
+    for there, group in zip(all_lanes, pair_groups):
+        theirs = 2 * there + 1 - core
+        group.start(dq_own_base.at[theirs], dq_pair_base.at[there], partner)
+        pair_tail_group.start(dq_own_tail.at[theirs], dq_pair_tail.at[there], partner)
     found_group.done(found_land.at[pl.ds(0, plane - 1)])
     found = jnp.sum(found_land[...][:, 0], axis=0, keepdims=True)
     loss_land[row] = jnp.broadcast_to(
@@ -498,6 +526,33 @@
     loss_group = groups.new()
     for device in line_peers:
         loss_group.start(loss_land.at[row], loss_land.at[row], device)
+    dq_group, dq_tail_group = groups.new(), groups.new()
+    for there, group in zip(all_lanes, pair_groups):
+        group.done(dq_pair_base.at[there])
+        total = dq_own_base[2 * there + core] + dq_pair_base[there]
+        if there is lane:
+            dq_mine = total
+        else:
+            dq_out_base[there] = total.astype(BF16)
+            device = row * plane + 2 * there + core
+            dq_group.start(dq_out_base.at[there], dq_land_base.at[lane], device)
+    pair_tail_group.done(dq_pair_tail.at[pl.ds(0, lanes)])
+    for there in lane_others:
+        dq_out_tail[there] = (dq_own_tail[2 * there + core] + dq_pair_tail[there]).astype(BF16)
+        device = row * plane + 2 * there + core
+        dq_tail_group.start(dq_out_tail.at[there], dq_land_tail.at[lane], device)
+    dq_mine_tail = dq_own_tail[2 * lane + core] + dq_pair_tail[lane]
+    if relayed:
+        for at, far in ((1, 3), (2, 0)):
+
+            @pl.when(row == at)
+            def _():
+                relay_group.landed(dp_relay_base)
+                relay_tail_group.landed(dp_relay_tail)
+                dp_out_base[far] = (dp_own_base[far] + dp_relay_base[...].astype(F32)).astype(BF16)
+                dp_out_tail[far] = (dp_own_tail[far] + dp_relay_tail[...].astype(F32)).astype(BF16)
+                send_dp(far, far, at)
+
     pair_base.done(feat_base.at[0])
     pair_tail.done(feat_tail.at[0])
     x_rows = 4 * base
@@ -508,9 +563,13 @@
         hidden, slope = gelu_and_slope(dot(all_x[...], w_first[:, pl.ds(start, tile)], 1, 0))
         all_hidden[t] = hidden.astype(BF16)
         all_slope[t] = slope
-    finish_dq()
-    de_base[core, 0] = gathered(dq_own_base, dq_land_base, spot, plane)
-    de_tail[core, 0] = gathered(dq_own_tail, dq_land_tail, spot, plane)
+    dq_group.done(dq_land_base.at[pl.ds(0, lanes - 1)])
+    dq_tail_group.done(dq_land_tail.at[pl.ds(0, lanes - 1)])
+    for there in lane_others:
+        dq_mine = dq_mine + dq_land_base[there].astype(F32)
+        dq_mine_tail = dq_mine_tail + dq_land_tail[there].astype(F32)
+    de_base[core, 0] = dq_mine.astype(BF16)
+    de_tail[core, 0] = dq_mine_tail.astype(BF16)
 
     def send_de(side):
         base_group, tail_group = groups.new(), groups.new()
@@ -524,16 +583,35 @@
         return finish
 
     finish_pair = [send_de(0)]
-    finish_dp()
-    de_base[core, 1] = gathered(dp_own_base, dp_land_base, row, rows)
-    de_tail[core, 1] = gathered(dp_own_tail, dp_land_tail, row, rows)
+    def dp_landed(count):
+        dp_group.done(dp_land_base.at[pl.ds(0, count)])
+        dp_tail_group.done(dp_land_tail.at[pl.ds(0, count)])
+
+    if relayed:
+        ends = lax.rem(row, 3) == 0
+
+        @pl.when(ends)
+        def _():
+            dp_landed(2)
+            relay_group.sent(dp_relay_base)
+            relay_tail_group.sent(dp_relay_tail)
+
+        @pl.when(jnp.logical_not(ends))
+        def _():
+            dp_landed(3)
+    else:
+        dp_landed(rows - 1)
+    dp_mine, dp_mine_tail = dp_own_base[row], dp_own_tail[row]
+    for k in range(1, rows):
+        there = lax.rem(row + k, rows)
+        part, part_tail = dp_land_base[there].astype(F32), dp_land_tail[there].astype(F32)
+        if relayed:
+            used = jnp.logical_not(jnp.logical_and(ends, row + there == 3))
+            part, part_tail = jnp.where(used, part, 0.0), jnp.where(used, part_tail, 0.0)
+        dp_mine, dp_mine_tail = dp_mine + part, dp_mine_tail + part_tail
+    de_base[core, 1] = dp_mine.astype(BF16)
+    de_tail[core, 1] = dp_mine_tail.astype(BF16)
     finish_pair.append(send_de(1))
-    loss_group.done(loss_land.at[pl.ds(0, rows - 1)])
-    loss = loss_land[0]
-    for k in range(1, rows):
-        loss = loss + loss_land[k]
-    out_loss[...] = loss * (1.0 / (size * spare))
-
     low_count, high_count = 2, lanes // 2
     low_lane, high_lane = lax.rem(lane, low_count), lax.div(lane, low_count)
     low_others = [lax.rem(low_lane + k, low_count) for k in range(1, low_count)]
@@ -707,6 +785,11 @@
         sender = plane * sender_row + column + sender_core
         total = total + jnp.where(sender == me, 0.0, landed[sender_row].astype(F32))
     out_all[...] = total
+    loss_group.done(loss_land.at[pl.ds(0, rows - 1)])
+    loss = loss_land[0]
+    for k in range(1, rows):
+        loss = loss + loss_land[k]
+    out_loss[...] = loss * (1.0 / (size * spare))
 
 
 def split_kernel(loss, total, mean_loss, first, second):
@@ -744,7 +827,7 @@
     block = base + unit
     vmem = pl.BlockSpec(memory_space=pltpu.VMEM)
     anywhere = pl.BlockSpec(memory_space=pl.ANY)
-    count = 20 + rows + lanes + 2 * TILES * (1 + width // embed)
+    count = 26 + rows + 2 * lanes + 2 * TILES * (1 + width // embed)
 
     def split(members, dtype):
         return [
@@ -753,15 +836,20 @@
         ]
 
     scratch = [
-        pltpu.VMEM((rows, 16 // rows, unit, 2 * width), BF16),
-        pltpu.VMEM((16 // rows, rows, unit, 2 * width), BF16),
+        pltpu.VMEM((rows, 16 // rows, unit, width), BF16),
+        pltpu.VMEM((rows, 16 // rows, unit, width), BF16),
+        pltpu.VMEM((16 // rows, rows, unit, width), BF16),
+        pltpu.VMEM((16 // rows, rows, unit, width), BF16),
         pltpu.VMEM((rows, unit, 2 * width), BF16),
         pltpu.VMEM((rows, unit, 2 * width), BF16),
         pltpu.VMEM((16,) + positives.shape, F32),
         pltpu.VMEM((2, 2, base, width), BF16),
         pltpu.VMEM((2, 2, unit, width), BF16),
-        *split(plane, BF16),
+        pltpu.VMEM((plane, base, embed), BF16),
         pltpu.VMEM((rows, base, embed), BF16),
+        pltpu.VMEM((plane, unit, embed), BF16),
+        pltpu.VMEM((rows, 16 // rows, unit, embed), BF16),
+        pltpu.VMEM((16 // rows, rows, unit, embed), BF16),
         pltpu.VMEM((rows, unit, embed), BF16),
         pltpu.VMEM((rows, unit, embed), BF16),
         pltpu.VMEM((rows, rows * unit, embed), BF16),
@@ -772,11 +860,14 @@
         pltpu.VMEM((plane, 2, plane * block), F32),
         pltpu.VMEM((plane, 1, plane * block), F32),
         *split(plane, F32),
-        *split(plane, BF16),
-        *split(plane, BF16),
+        *split(lanes, F32),
+        *split(lanes, BF16),
+        *split(lanes, BF16),
         *split(rows, F32),
         *split(rows, BF16),
         *split(rows, BF16),
+        pltpu.VMEM((base, embed), BF16),
+        pltpu.VMEM((unit, embed), BF16),
         pltpu.VMEM((rows, 8, 128), F32),
         pltpu.VMEM((2, 2, base, embed), BF16),
         pltpu.VMEM((2, 2, unit, embed), BF16),

time: 64.3 us -> 62.5 us (0.972)
  Pallas kernels: 63.4 us -> 61.3 us
    pallas_call x1, Pallas kernels: 61.8 us -> 59.7 us  [step(): pl.pallas_call(functools.partial(step_kernel, size, plane, score_scale),...]
where the time goes in v3:
time: 62.5 us; the launch traced here: 62.1 us
  Pallas kernels  61.3 us (98%)
  between operations  0.8 us (1%)
    pallas_call x1, Pallas kernels, step(): pl.pallas_call(functools.partial(step_kernel, size, plane, score_scale),...  59.7 us
    pallas_call x1, Pallas kernels, split_outputs(): pl.pallas_call(split_kernel, out_shape=[jax.ShapeDtypeStruct((1,), F32),...  1.65 us

profile of v3, /device:TPU:9, one launch (start us, length us, event | category | flops | bytes accessed | tf_op | source)
XLA Modules:
  0.0 62.1 jit_solution(922731882237971523)
XLA Ops:
  0.6 59.7 %shard_map.85 = (f32[8,128]{1,0:T(8,128)}, f32[48,1152]{1,0:T(8,128)}) custom-call(s32[32]{0:T(128)} %counts.1, bf16[256,768]{1,0:T(8,128)(2,1)} %query_hbm.1, bf16[256,768]{1,0:T(8,128)(2,1)} %passage_hbm.1, s32[1,256]{1,0:T(1,128)} %bitcast.3, bf16[768,1536]{1,0:T(8,128)(2,1)} %w_first_hbm.1, bf16[1536,384]{1,0:T(8,128)(2,1)} %w_second_hbm.1), custom_call_target="tpu_custom_call" | custom-call | tf_op jit(solution)/shard_map/pallas_call | solution.py:893
  60.3 1.6 %shard_map.86 = (f32[1]{0:T(128)}, f32[48,768]{1,0:T(8,128)}, f32[48,384]{1,0:T(8,128)}) custom-call(f32[8,128]{1,0:T(8,128)} %get-tuple-element.8.loss, f32[48,1152]{1,0:T(8,128)} %get-tuple-element.9.total), custom_call_target="tpu_custom_call" | custom-call | tf_op jit(solution)/shard_map/pallas_call | solution.py:805

commit v4 on v3

--- a/solution.py
+++ b/solution.py
@@ -15,6 +15,8 @@
 TILES = 2
 AHEAD = 3
 DELAY = 2
+LAST = 128
+BEHIND = 0
 
 
 def gelu_and_slope(value):
@@ -132,6 +134,7 @@
     landing,
     outgoing_two,
     landing_two,
+    landing_direct,
     sums,
     forward,
     landed,
@@ -561,7 +564,7 @@
     for t in range(TILES):
         start = pl.multiple_of(core * hidden_half + t * tile, 128)
         hidden, slope = gelu_and_slope(dot(all_x[...], w_first[:, pl.ds(start, tile)], 1, 0))
-        all_hidden[t] = hidden.astype(BF16)
+        all_hidden[t] = hidden.T.astype(BF16)
         all_slope[t] = slope
     dq_group.done(dq_land_base.at[pl.ds(0, lanes - 1)])
     dq_tail_group.done(dq_land_tail.at[pl.ds(0, lanes - 1)])
@@ -621,8 +624,14 @@
     def in_plane(high, low):
         return plane * row + 2 * (high * low_count + low) + core
 
+    direct = []
+
+    def tile_of(t):
+        return t + core * (TILES - 1 - 2 * t)
+
     def first_stage(chunk_at, part):
         t, cols = chunk_at
+        t = tile_of(t)
         for i in range(per_tile):
             for high in range(high_count):
                 for low in range(low_count):
@@ -637,6 +646,22 @@
                             slot = skip + (high * half + step) * low_count + low
                         outgoing[slot, :, cols] = piece.astype(BF16)
         group = groups.new()
+        if chunk_at in direct:
+            for away in lane_others:
+                high, low = lax.div(away, low_count), lax.rem(away, low_count)
+                for i in range(per_tile):
+                    step = t * per_tile + i
+                    slots = (
+                        (low * half + step) * high_count + high,
+                        skip + (high * half + step) * low_count + low,
+                    )
+                    for j in range(2):
+                        group.start(
+                            outgoing.at[slots[j], :, cols],
+                            landing_direct.at[(lane * half + step) * 2 + j],
+                            in_plane(high, low),
+                        )
+            return group
         span = per_tile * high_count
         for low in low_others:
             group.start(
@@ -655,9 +680,10 @@
 
     def second_stage(chunk_at, before):
         t, cols = chunk_at
+        t = tile_of(t)
         count = (low_count - 1) * high_count + (high_count - 1) * low_count
         before.done(landing.at[pl.ds(0, per_tile * count), :, cols])
-        for i in range(t * per_tile, (t + 1) * per_tile):
+        for i in [t * per_tile + n for n in range(per_tile)]:
             for high in range(high_count):
                 total = own[i, 0, high, low_lane, :, cols]
                 for low in low_others:
@@ -699,17 +725,23 @@
 
     def third_stage(chunk_at, before):
         t, cols = chunk_at
-        count = low_count - 1 + high_count - 1
-        before.done(landing_two.at[pl.ds(0, per_tile * count), :, cols])
-        for i in range(t * per_tile, (t + 1) * per_tile):
+        t = tile_of(t)
+        if chunk_at in direct:
+            before.done(landing_direct.at[pl.ds(0, (lanes - 1) * per_tile * 2)])
+        else:
+            count = low_count - 1 + high_count - 1
+            before.done(landing_two.at[pl.ds(0, per_tile * count), :, cols])
+        for i in [t * per_tile + n for n in range(per_tile)]:
             for j in range(2):
                 total = own[i, j, high_lane, low_lane, :, cols]
-                if j == 0:
-                    slots = [high * half + i for high in high_others]
+                if chunk_at in direct:
+                    parts = [landing_direct[(away * half + i) * 2 + j] for away in lane_others]
+                elif j == 0:
+                    parts = [landing_two[high * half + i, :, cols] for high in high_others]
                 else:
-                    slots = [skip_two + low * half + i for low in low_others]
-                for slot in slots:
-                    total = total + landing_two[slot, :, cols].astype(F32)
+                    parts = [landing_two[skip_two + low * half + i, :, cols] for low in low_others]
+                for landed_part in parts:
+                    total = total + landed_part.astype(F32)
                 sums[i, j, :, cols] = total
                 forward[i, j, :, cols] = total.astype(BF16)
 
@@ -725,11 +757,12 @@
     def part_of(chunk_at):
         t, cols = chunk_at
         if cols.start >= width:
-            return dot(all_hidden[t], de[:, cols.start - width : cols.start - width + cols.size], 0, 0)
+            low = cols.start - width
+            return dot(all_hidden[tile_of(t)], de[:, low : low + cols.size], 1, 0)
         if t not in act_grads:
-            start = pl.multiple_of(core * hidden_half + t * tile, 128)
+            start = pl.multiple_of(core * hidden_half + tile_of(t) * tile, 128)
             back = dot(de, w_second[pl.ds(start, tile), :], 1, 1)
-            act_grads[t] = (all_slope[t] * back).astype(BF16)
+            act_grads[t] = (all_slope[tile_of(t)] * back).astype(BF16)
         return dot(act_grads[t], all_x[:, cols], 0, 0)
 
     piece = embed
@@ -738,14 +771,19 @@
         chunks.append((t, pl.ds(width, piece)))
         for low in range(0, width, piece):
             chunks.append((t, pl.ds(low, piece)))
+    chunks[-1:] = [(TILES - 1, pl.ds(width - piece, piece - LAST))] if LAST < piece else []
+    direct.append((TILES - 1, pl.ds(width - LAST, LAST)))
     ones, twos = [], []
     for at in range(len(chunks) + DELAY):
         if at < len(chunks):
             for ahead in range(len(ones), min(at + AHEAD, len(chunks))):
                 ones.append(first_stage(chunks[ahead], part_of(chunks[ahead])))
+            if at == len(chunks) - 1 - BEHIND:
+                last = first_stage(direct[0], part_of(direct[0]))
             twos.append(second_stage(chunks[at], ones[at]))
         if at >= DELAY:
             third_stage(chunks[at - DELAY], twos[at - DELAY])
+    third_stage(direct[0], last)
 
     if relayed:
         for at in range(rows):
@@ -877,6 +915,7 @@
         pltpu.VMEM((2 * half * lanes, chunk, across), BF16),
         pltpu.VMEM((half * (lanes // 2 + 2), chunk, across), BF16),
         pltpu.VMEM((half * (lanes // 2 + 2), chunk, across), BF16),
+        pltpu.VMEM((2 * half * lanes, chunk, LAST), BF16),
         pltpu.VMEM((half, 2, chunk, across), F32),
         pltpu.VMEM((half, 2, chunk, across), BF16),
         pltpu.VMEM((rows, chunk, across), BF16),
@@ -886,7 +925,7 @@
         pltpu.SemaphoreType.DMA((rows,)),
         pltpu.VMEM(w_first.shape, BF16),
         pltpu.VMEM(w_second.shape, BF16),
-        pltpu.VMEM((TILES, 4 * block, hidden_width // 2 // TILES), BF16),
+        pltpu.VMEM((TILES, hidden_width // 2 // TILES, 4 * block), BF16),
         pltpu.VMEM((TILES, 4 * block, hidden_width // 2 // TILES), F32),
         pltpu.SemaphoreType.DMA((6,)),
     ]

time: 62.5 us -> 62 us (level)
  no operation moved by 1% of the time
where the time goes in v4:
time: 62 us; the launch traced here: 61.7 us
  Pallas kernels  60.9 us (98%)
  between operations  0.8 us (1%)
    pallas_call x1, Pallas kernels, step(): pl.pallas_call(functools.partial(step_kernel, size, plane, score_scale),...  59.2 us
    pallas_call x1, Pallas kernels, split_outputs(): pl.pallas_call(split_kernel, out_shape=[jax.ShapeDtypeStruct((1,), F32),...  1.65 us

profile of v4, /device:TPU:9, one launch (start us, length us, event | category | flops | bytes accessed | tf_op | source)
XLA Modules:
  0.0 61.7 jit_solution(5616497935751377120)
XLA Ops:
  0.6 59.2 %shard_map.85 = (f32[8,128]{1,0:T(8,128)}, f32[48,1152]{1,0:T(8,128)}) custom-call(s32[32]{0:T(128)} %counts.1, bf16[256,768]{1,0:T(8,128)(2,1)} %query_hbm.1, bf16[256,768]{1,0:T(8,128)(2,1)} %passage_hbm.1, s32[1,256]{1,0:T(1,128)} %bitcast.3, bf16[768,1536]{1,0:T(8,128)(2,1)} %w_first_hbm.1, bf16[1536,384]{1,0:T(8,128)(2,1)} %w_second_hbm.1), custom_call_target="tpu_custom_call" | custom-call | tf_op jit(solution)/shard_map/pallas_call | solution.py:932
  59.9 1.6 %shard_map.86 = (f32[1]{0:T(128)}, f32[48,768]{1,0:T(8,128)}, f32[48,384]{1,0:T(8,128)}) custom-call(f32[8,128]{1,0:T(8,128)} %get-tuple-element.8.loss, f32[48,1152]{1,0:T(8,128)} %get-tuple-element.9.total), custom_call_target="tpu_custom_call" | custom-call | tf_op jit(solution)/shard_map/pallas_call | solution.py:843

commit v5 on v4

--- a/solution.py
+++ b/solution.py
@@ -66,7 +66,12 @@
 
 class Groups:
     def __init__(self, send, recv):
-        self.send, self.recv, self.used = send, recv, 0
+        self.send, self.recv, self.used, self.alone = send, recv, 0, 0
+
+    def new_recv(self):
+        self.alone += 1
+        assert self.used + self.alone <= self.recv.shape[0]
+        return self.recv.at[self.recv.shape[0] - self.alone]
 
     def new(self):
         self.used += 1
@@ -625,6 +630,10 @@
         return plane * row + 2 * (high * low_count + low) + core
 
     direct = []
+    stage_send = load_sems.at[6]
+
+    def stage_group():
+        return Group(stage_send, groups.new_recv())
 
     def tile_of(t):
         return t + core * (TILES - 1 - 2 * t)
@@ -645,7 +654,7 @@
                         else:
                             slot = skip + (high * half + step) * low_count + low
                         outgoing[slot, :, cols] = piece.astype(BF16)
-        group = groups.new()
+        group = stage_group()
         if chunk_at in direct:
             for away in lane_others:
                 high, low = lax.div(away, low_count), lax.rem(away, low_count)
@@ -682,7 +691,7 @@
         t, cols = chunk_at
         t = tile_of(t)
         count = (low_count - 1) * high_count + (high_count - 1) * low_count
-        before.done(landing.at[pl.ds(0, per_tile * count), :, cols])
+        before.landed(landing.at[pl.ds(0, per_tile * count), :, cols])
         for i in [t * per_tile + n for n in range(per_tile)]:
             for high in range(high_count):
                 total = own[i, 0, high, low_lane, :, cols]
@@ -697,7 +706,7 @@
                     total = total + landing[slot, :, cols].astype(F32)
                 own[i, 1, high_lane, low, :, cols] = total
                 outgoing_two[skip_two + low * half + i, :, cols] = total.astype(BF16)
-        group = groups.new()
+        group = stage_group()
         block = t * per_tile
         for high in high_others:
             group.start(
@@ -727,10 +736,10 @@
         t, cols = chunk_at
         t = tile_of(t)
         if chunk_at in direct:
-            before.done(landing_direct.at[pl.ds(0, (lanes - 1) * per_tile * 2)])
+            before.landed(landing_direct.at[pl.ds(0, (lanes - 1) * per_tile * 2)])
         else:
             count = low_count - 1 + high_count - 1
-            before.done(landing_two.at[pl.ds(0, per_tile * count), :, cols])
+            before.landed(landing_two.at[pl.ds(0, per_tile * count), :, cols])
         for i in [t * per_tile + n for n in range(per_tile)]:
             for j in range(2):
                 total = own[i, j, high_lane, low_lane, :, cols]
@@ -784,6 +793,8 @@
         if at >= DELAY:
             third_stage(chunks[at - DELAY], twos[at - DELAY])
     third_stage(direct[0], last)
+    all_sent = landing.at[pl.ds(0, 2 * half * (lanes - 1))]
+    pltpu.make_async_copy(all_sent, all_sent, stage_send).wait()
 
     if relayed:
         for at in range(rows):
@@ -865,7 +876,8 @@
     block = base + unit
     vmem = pl.BlockSpec(memory_space=pltpu.VMEM)
     anywhere = pl.BlockSpec(memory_space=pl.ANY)
-    count = 26 + rows + 2 * lanes + 2 * TILES * (1 + width // embed)
+    count = 25 + rows + 2 * lanes
+    alone = 2 * TILES * (1 + width // embed) + 1
 
     def split(members, dtype):
         return [
@@ -920,14 +932,14 @@
         pltpu.VMEM((half, 2, chunk, across), BF16),
         pltpu.VMEM((rows, chunk, across), BF16),
         pltpu.SemaphoreType.DMA((count,)),
-        pltpu.SemaphoreType.DMA((count,)),
+        pltpu.SemaphoreType.DMA((count + alone,)),
         pltpu.SemaphoreType.DMA((half, 2)),
         pltpu.SemaphoreType.DMA((rows,)),
         pltpu.VMEM(w_first.shape, BF16),
         pltpu.VMEM(w_second.shape, BF16),
         pltpu.VMEM((TILES, hidden_width // 2 // TILES, 4 * block), BF16),
         pltpu.VMEM((TILES, 4 * block, hidden_width // 2 // TILES), F32),
-        pltpu.SemaphoreType.DMA((6,)),
+        pltpu.SemaphoreType.DMA((7,)),
     ]
     return pl.pallas_call(
         functools.partial(step_kernel, size, plane, score_scale),

time: 62 us -> 61.9 us (level)
  no operation moved by 1% of the time
where the time goes in v5:
time: 61.9 us; the launch traced here: 61.6 us
  Pallas kernels  60.8 us (98%)
  between operations  0.8 us (1%)
    pallas_call x1, Pallas kernels, step(): pl.pallas_call(functools.partial(step_kernel, size, plane, score_scale),...  59.1 us
    pallas_call x1, Pallas kernels, split_outputs(): pl.pallas_call(split_kernel, out_shape=[jax.ShapeDtypeStruct((1,), F32),...  1.65 us

profile of v5, /device:TPU:9, one launch (start us, length us, event | category | flops | bytes accessed | tf_op | source)
XLA Modules:
  0.0 61.6 jit_solution(7516047635203641653)
XLA Ops:
  0.6 59.1 %shard_map.85 = (f32[8,128]{1,0:T(8,128)}, f32[48,1152]{1,0:T(8,128)}) custom-call(s32[32]{0:T(128)} %counts.1, bf16[256,768]{1,0:T(8,128)(2,1)} %query_hbm.1, bf16[256,768]{1,0:T(8,128)(2,1)} %passage_hbm.1, s32[1,256]{1,0:T(1,128)} %bitcast.3, bf16[768,1536]{1,0:T(8,128)(2,1)} %w_first_hbm.1, bf16[1536,384]{1,0:T(8,128)(2,1)} %w_second_hbm.1), custom_call_target="tpu_custom_call" | custom-call | tf_op jit(solution)/shard_map/pallas_call | solution.py:944
  59.8 1.6 %shard_map.86 = (f32[1]{0:T(128)}, f32[48,768]{1,0:T(8,128)}, f32[48,384]{1,0:T(8,128)}) custom-call(f32[8,128]{1,0:T(8,128)} %get-tuple-element.8.loss, f32[48,1152]{1,0:T(8,128)} %get-tuple-element.9.total), custom_call_target="tpu_custom_call" | custom-call | tf_op jit(solution)/shard_map/pallas_call | solution.py:854
